TPU v7x, 64 devices: a 2x2x8 block of a 4x4x8 slice. The times are simulated.
64 devices in a mesh: dp: 4 (over x, y), tp: 16 (over z, core).
Axes of the slice: x: 2, y: 2, z: 8, core: 2. Of those that a mesh axis runs over, the one named last changes fastest.
The devices are a block of a 4x4x8 slice.
Arguments:
- x_in: bfloat16 [4096, 6144], P(('dp', 'tp')), parts along dimension 0
- grad_out: bfloat16 [4096, 6144], P(('dp', 'tp')), parts along dimension 0
- positions: int32 [4096], P('dp'), parts along dimension 0
- norm_gain: float32 [6144], replicated
- w_query: bfloat16 [6144, 6144], P(None, 'tp')
- w_key: bfloat16 [6144, 1024], replicated
- w_value: bfloat16 [6144, 1024], replicated
- w_out: bfloat16 [6144, 6144], P('tp')
Outputs:
- output 1: bfloat16 [4096, 6144], P(('dp', 'tp')), parts along dimension 0
- output 2: bfloat16 [4096, 6144], P(('dp', 'tp')), parts along dimension 0
- output 3: bfloat16 [24576, 6144], P('dp', 'tp'), parts along dimension 0
- output 4: float32 [24576, 2048], P('dp', 'tp'), parts along dimension 0
- output 5: float32 [24576, 2048], P('dp', 'tp'), parts along dimension 0
- output 6: bfloat16 [24576, 6144], P(('dp', 'tp')), parts along dimension 0
- output 7: float32 [24576], P('dp'), parts along dimension 0
There are 4 independent parts. A program takes and returns all parts, laid end to end along the dimension named above; an argument that names none is the same for every part.
All inputs are finite; a program needn't handle non-finite values.
Results may differ from a plain program's by a relative error of at most 0.02.
Values are sent between devices in bfloat16 or wider.
A program may use at most 768 MiB of HBM per device.

v0:
```python
import functools
import jax
import jax.numpy as jnp
from jax import lax
from jax.sharding import PartitionSpec as P

HEAD_DIM = 128
QUERY_BLOCK = 256
SCORE_SCALE = HEAD_DIM ** -0.5
ROPE_THETA = 1000000.0
NORM_EPS = 1e-05


def rope_tables(positions):
    exponents = jnp.arange(0, HEAD_DIM, 2, dtype=jnp.float32) / HEAD_DIM
    angles = positions.astype(jnp.float32)[..., None] * jnp.power(ROPE_THETA, -exponents)
    return jnp.cos(angles), jnp.sin(angles)


def apply_rope(tensor, cos_t, sin_t):
    half_dim = HEAD_DIM // 2
    t_f32 = tensor.astype(jnp.float32)
    lead_half = t_f32[..., :half_dim]
    tail_half = t_f32[..., half_dim:]
    return jnp.concatenate([lead_half * cos_t - tail_half * sin_t, tail_half * cos_t + lead_half * sin_t], axis=-1).astype(jnp.bfloat16)


def norm_forward(x_f32, norm_gain):
    inv_rms = lax.rsqrt(jnp.mean(x_f32 * x_f32, axis=-1, keepdims=True) + NORM_EPS)
    x_hat = x_f32 * inv_rms
    return (x_hat * norm_gain).astype(jnp.bfloat16), x_hat, inv_rms


def norm_backward(d_hidden, x_hat, inv_rms, norm_gain):
    d_f32 = d_hidden.astype(jnp.float32)
    d_gain = jnp.sum(d_f32 * x_hat, axis=-2)
    value_a6 = d_f32 * norm_gain
    d_input = inv_rms * (value_a6 - x_hat * jnp.mean(value_a6 * x_hat, axis=-1, keepdims=True))
    return d_input, d_gain


def attend(positions, q_raw, k_raw, v_raw):
    seq_len, heads_loc = q_raw.shape[0], q_raw.shape[1]
    cos_t, sin_t = rope_tables(positions)
    q_rot = apply_rope(q_raw, cos_t[:, None, :], sin_t[:, None, :])
    k_rot = apply_rope(k_raw, cos_t, sin_t)
    col_idx = lax.iota(jnp.int32, seq_len)
    key_doc = positions - col_idx
    num_blk = seq_len // QUERY_BLOCK

    def one_block(blk_item):
        q_blk, q_pos, row_idx = blk_item
        scores = jnp.einsum('qhd,sd->hqs', q_blk, k_rot, preferred_element_type=jnp.float32) * SCORE_SCALE
        keep_mask = (col_idx[None, :] <= row_idx[:, None]) & (key_doc[None, :] == (q_pos - row_idx)[:, None])
        scores = jnp.where(keep_mask[None], scores, -1e30)
        prob_blk = jax.nn.softmax(scores, axis=-1).astype(jnp.bfloat16)
        return jnp.einsum('hqs,sd->qhd', prob_blk, v_raw, preferred_element_type=jnp.float32).astype(jnp.bfloat16)

    blk_out = lax.map(jax.checkpoint(one_block), (q_rot.reshape(num_blk, QUERY_BLOCK, heads_loc, HEAD_DIM), positions.reshape(num_blk, QUERY_BLOCK), col_idx.reshape(num_blk, QUERY_BLOCK)))
    return blk_out.reshape(seq_len, heads_loc, HEAD_DIM)


def share_sum(part_val, tp_size, kv_repeat):
    summed = part_val
    for offset in range(1, kv_repeat):
        pair_perm = [(src_dev, (src_dev // kv_repeat) * kv_repeat + (src_dev + offset) % kv_repeat) for src_dev in range(tp_size)]
        summed = summed + lax.ppermute(part_val, 'tp', pair_perm)
    return summed


def solution(mesh):
    tp_size = mesh.shape['tp']
    contract_rows = (((0,), (0,)), ((), ()))
    contract_cols = (((1,), (1,)), ((), ()))

    def device_step(x_blk, dy_blk, pos_all, norm_gain, wq_loc, wk_all, wv_all, wo_loc):
        kv_heads = wk_all.shape[1] // HEAD_DIM
        kv_repeat = tp_size // kv_heads
        heads_loc = wq_loc.shape[1] // HEAD_DIM
        kv_index = lax.axis_index('tp') // kv_repeat
        wk_loc = lax.dynamic_slice_in_dim(wk_all, kv_index * HEAD_DIM, HEAD_DIM, axis=1)
        wv_loc = lax.dynamic_slice_in_dim(wv_all, kv_index * HEAD_DIM, HEAD_DIM, axis=1)
        x_f32 = x_blk.astype(jnp.float32)
        hidden, x_hat, inv_rms = norm_forward(x_f32, norm_gain)
        h_full = lax.all_gather(hidden, 'tp', axis=0, tiled=True)
        seq_len = h_full.shape[0]
        q_raw = jnp.dot(h_full, wq_loc, preferred_element_type=jnp.float32).astype(jnp.bfloat16)
        k_raw = jnp.dot(h_full, wk_loc, preferred_element_type=jnp.float32).astype(jnp.bfloat16)
        v_raw = jnp.dot(h_full, wv_loc, preferred_element_type=jnp.float32).astype(jnp.bfloat16)
        attn_out, attn_pull = jax.vjp(functools.partial(attend, pos_all), q_raw.reshape(seq_len, heads_loc, HEAD_DIM), k_raw, v_raw)
        o_flat = attn_out.reshape(seq_len, heads_loc * HEAD_DIM)
        mix_part = jnp.dot(o_flat, wo_loc, preferred_element_type=jnp.float32).astype(jnp.bfloat16)
        mix_rows = lax.psum_scatter(mix_part, 'tp', scatter_dimension=0, tiled=True)
        result = (x_f32 + mix_rows.astype(jnp.float32)).astype(jnp.bfloat16)
        dy_full = lax.all_gather(dy_blk, 'tp', axis=0, tiled=True)
        d_wo = lax.dot_general(o_flat, dy_full, contract_rows, preferred_element_type=jnp.float32).astype(jnp.bfloat16)
        d_o = lax.dot_general(dy_full, wo_loc, contract_cols, preferred_element_type=jnp.float32).astype(jnp.bfloat16)
        d_q, d_k, d_v = attn_pull(d_o.reshape(seq_len, heads_loc, HEAD_DIM))
        dq_flat = d_q.reshape(seq_len, heads_loc * HEAD_DIM)
        d_wq = lax.dot_general(h_full, dq_flat, contract_rows, preferred_element_type=jnp.float32).astype(jnp.bfloat16)
        dwk_part = lax.dot_general(h_full, d_k, contract_rows, preferred_element_type=jnp.float32)
        dwv_part = lax.dot_general(h_full, d_v, contract_rows, preferred_element_type=jnp.float32)
        dh_part = (lax.dot_general(dq_flat, wq_loc, contract_cols, preferred_element_type=jnp.float32) + lax.dot_general(d_k, wk_loc, contract_cols, preferred_element_type=jnp.float32) + lax.dot_general(d_v, wv_loc, contract_cols, preferred_element_type=jnp.float32)).astype(jnp.bfloat16)
        dh_rows = lax.psum_scatter(dh_part, 'tp', scatter_dimension=0, tiled=True)
        d_input, dg_part = norm_backward(dh_rows, x_hat, inv_rms, norm_gain)
        grad_x = (dy_blk.astype(jnp.float32) + d_input).astype(jnp.bfloat16)
        d_gain = lax.psum(dg_part, 'tp')
        d_wk = share_sum(dwk_part, tp_size, kv_repeat)
        d_wv = share_sum(dwv_part, tp_size, kv_repeat)
        return result, grad_x, d_wq, d_wk, d_wv, d_wo, d_gain

    specs_in = (P(('dp', 'tp'), None), P(('dp', 'tp'), None), P('dp'), P(), P(None, 'tp'), P(), P(), P('tp', None))
    specs_out = (P(('dp', 'tp'), None), P(('dp', 'tp'), None), P('dp', 'tp'), P('dp', 'tp'), P('dp', 'tp'), P(('dp', 'tp'), None), P('dp'))
    return jax.shard_map(device_step, mesh=mesh, in_specs=specs_in, out_specs=specs_out, check_vma=False)
```

profile of v0, /device:TPU:21, one launch (start us, length us, event | category | flops | bytes accessed | tf_op | source)
XLA Modules:
  0.0 463.3 jit_solution(7181284470267742255)
XLA Ops:
  12.6 76.4 %all-gather.3.cloned.1.call-done = bf16[1024,6144]{1,0:T(8,128)(2,1)} async-done(((bf16[64,6144]{1,0:T(8,128)(2,1)}), bf16[1024,6144]{1,0:T(8,128)(2,1)}) %all-gather.3.cloned.1.call-update) | async-done | bytes 12582928 | tf_op jit(solution)/shard_map/all_gather | solution.py:85
  89.0 9.3 %fusion.90 = f32[1024,128]{0,1:T(8,128)S(1)} fusion(bf16[1024,6144]{1,0:T(8,128)(2,1)} %all-gather.3.cloned.1.call-done, bf16[6144,1024]{1,0:T(8,128)(2,1)} %param.17, s32[]{:T(128)S(6)} %select_n.49), kind=kOutput, calls=%fused_computation.111 | convolution fusion | flops 1610874880 | bytes 14680068 | tf_op jit(solution)/shard_map/dot_general | solution.py:88
  101.8 59.6 %all-gather.5.cloned.1.call-done = bf16[1024,6144]{1,0:T(8,128)(2,1)} async-done(((bf16[64,6144]{1,0:T(8,128)(2,1)}), bf16[1024,6144]{1,0:T(8,128)(2,1)}) %all-gather.5.cloned.1.call-update) | async-done | bytes 12582928 | tf_op jit(solution)/shard_map/all_gather | solution.py:95
  161.4 11.0 %convolution_convert_fusion.5 = bf16[1024,384]{1,0:T(8,128)(2,1)S(1)} fusion(bf16[1024,6144]{1,0:T(8,128)(2,1)} %all-gather.5.cloned.1.call-done, bf16[384,6144]{1,0:T(8,128)(2,1)} %param.19), kind=kOutput, calls=%fused_computation.100 | convolution fusion | flops 4832231424 | bytes 18087936 | tf_op jit(solution)/shard_map/dot_general | solution.py:97
  174.0 9.5 %convolution_convert_fusion.6 = bf16[1024,384]{0,1:T(8,128)(2,1)S(1)} fusion(bf16[1024,6144]{1,0:T(8,128)(2,1)} %all-gather.3.cloned.1.call-done, bf16[6144,384]{1,0:T(8,128)(2,1)} %param.16), kind=kOutput, calls=%fused_computation.101 | convolution fusion | flops 4832231424 | bytes 18087936 | tf_op jit(solution)/shard_map/dot_general | solution.py:87
  186.6 2.8 subtract_convert_fusion
  193.7 9.1 %fusion.93 = bf16[1024,128]{1,0:T(8,128)(2,1)} fusion(bf16[1024,6144]{1,0:T(8,128)(2,1)} %all-gather.3.cloned.1.call-done, bf16[6144,1024]{1,0:T(8,128)(2,1)} %param.18, s32[]{:T(128)S(6)} %select_n.49), kind=kOutput, calls=%fused_computation.112 | convolution fusion | flops 1610743808 | bytes 14417924 | tf_op jit(solution)/shard_map/dot_general | solution.py:89
  202.9 46.3 %while.32 = (s32[]{:T(128)}, bf16[1024,128]{1,0:T(8,128)(2,1)S(1)}, bf16[1024,128]{1,0:T(8,128)(2,1)}, bf16[4,256,3,128]{3,1,0,2:T(8,128)(2,1)S(1)}, bf16[4,256,...) while((s32[]{:T(128)}, bf16[1024,128]{1,0:T(8,128)(2,1)S(1)}, ...), condition=%wide.region_10.11_spmd.clone, body=%wide.region_6.10_spmd.clone.sunk | while | flops 1032454400 | bytes 29110448 | solution.py:59
  217.4 3.0 fusion.187
  229.1 3.0 fusion.187
  232.1 2.5 fusion.184
  240.9 3.0 fusion.187
  252.8 13.2 %fusion.79 = f32[1024,6144]{1,0:T(8,128)} fusion(bf16[1024,128]{1,0:T(8,128)(2,1)} %get-tuple-element.335, bf16[6144,1024]{1,0:T(8,128)(2,1)} %param.18, s32[]{:T(128)S(6)} %select_n.49), kind=kOutput, calls=%fused_computation.102 | convolution fusion | flops 1610612736 | bytes 27000836 | tf_op jit(solution)/shard_map/dot_general | solution.py:103
  266.0 11.5 %fusion.83 = f32[1024,6144]{1,0:T(8,128)} fusion(bf16[6144,1024]{1,0:T(8,128)(2,1)} %param.17, s32[]{:T(128)S(6)} %select_n.49, f32[1024,64]{0,1:T(8,128)S(1)} %get-tuple-element.516, f32[1024,64]{0,1:T(8,128)S(1)} %get-tuple-element.515), kind=kOutput, calls=%fused_computation.106 | convolution fusion | flops 1610874880 | bytes 27262980 | tf_op jit(solution)/shard_map/dot_general | solution.py:103
  277.5 23.6 %add_convert_fusion = bf16[1024,6144]{1,0:T(8,128)(2,1)} fusion(f32[1024,6144]{1,0:T(8,128)} %fusion.79, f32[1024,6144]{1,0:T(8,128)} %fusion.83, bf16[1024,384]{0,1:T(8,128)(2,1)S(1)} %bitcast.227, bf16[6144,384]{1,0:T(8,128)(2,1)} %param.16), kind=kOutput, calls=%fused_computation.74 | convolution fusion | flops 4850712576 | bytes 68419584 | tf_op jit(solution)/shard_map/dot_general | solution.py:103
  301.2 23.4 %while.31 = (s32[]{:T(128)}, bf16[4,256,3,128]{3,1,2,0:T(8,128)(2,1)S(1)}, s32[4,256]{1,0:T(4,128)S(1)}, s32[1,1024]{1,0:T(1,128)S(1)}, s32[4,256]{1,0:T(4,128)S...) while((s32[]{:T(128)}, ...), condition=%wide.region_4.5_spmd.clone, body=%wide.region_1.4_spmd.clone.sunk | while | flops 408257792 | bytes 7753841 | solution.py:59
  301.8 2.9 fusion.174
  304.6 2.6 fusion.175
  307.6 2.9 fusion.174
  310.4 2.6 fusion.175
  313.4 2.9 fusion.174
  316.2 2.6 fusion.175
  319.2 2.9 fusion.174
  322.1 2.6 fusion.175
  325.5 12.0 %convolution_convert_fusion.2 = bf16[1024,6144]{1,0:T(8,128)(2,1)} fusion(bf16[1024,384]{0,1:T(8,128)(2,1)S(1)} %bitcast.237, bf16[384,6144]{1,0:T(8,128)(2,1)} %param.19), kind=kOutput, calls=%fused_computation.75 | convolution fusion | flops 4838129664 | bytes 18087936 | tf_op jit(solution)/shard_map/dot_general | solution.py:92
  337.6 6.6 %fusion.128 = f32[6144,128]{1,0:T(8,128)S(1)} fusion(bf16[1024,6144]{1,0:T(8,128)(2,1)} %all-gather.3.cloned.1.call-done, bf16[1024,128]{1,0:T(8,128)(2,1)} %get-tuple-element.335), kind=kOutput, calls=%fused_computation.148 | convolution fusion | flops 1610612736 | bytes 15990784 | tf_op jit(solution)/shard_map/dot_general | solution.py:102
  344.5 6.7 %fusion.110 = f32[6144,128]{1,0:T(8,128)S(1)} fusion(bf16[1024,6144]{1,0:T(8,128)(2,1)} %all-gather.3.cloned.1.call-done, f32[1024,64]{0,1:T(8,128)S(1)} %get-tuple-element.516, f32[1024,64]{0,1:T(8,128)S(1)} %get-tuple-element.515), kind=kOutput, calls=%fused_computation.133 | convolution fusion | flops 1610874880 | bytes 16252928 | tf_op jit(solution)/shard_map/dot_general | solution.py:101
  351.6 11.7 %convolution_convert_fusion.3 = bf16[384,6144]{1,0:T(8,128)(2,1)} fusion(bf16[1024,384]{0,1:T(8,128)(2,1)S(1)} %bitcast.238, bf16[1024,6144]{1,0:T(8,128)(2,1)} %all-gather.5.cloned.1.call-done), kind=kOutput, calls=%fused_computation.76 | convolution fusion | flops 4834197504 | bytes 18087936 | tf_op jit(solution)/shard_map/dot_general | solution.py:96
  363.3 8.6 %convolution_convert_fusion.4 = bf16[6144,384]{1,0:T(8,128)(2,1)} fusion(bf16[1024,6144]{1,0:T(8,128)(2,1)S(1)} %bitcast.226, bf16[1024,384]{0,1:T(8,128)(2,1)S(1)} %bitcast.228), kind=kOutput, calls=%fused_computation.77 | convolution fusion | flops 4834197504 | bytes 18087936 | tf_op jit(solution)/shard_map/dot_general | solution.py:100
  377.6 44.4 %psum.7 = f32[6144]{0:T(1024)} all-reduce(f32[6144]{0:T(1024)S(1)} %get-tuple-element.457), channel_id=1, replica_groups=mesh['dp'=4,'tp'=16] {'tp'}, use_global_device_ids=true, to_apply=%region_14.15 | all-reduce | flops 6144 | bytes 49152 | tf_op jit(solution)/shard_map/psum | solution.py:107
  422.0 31.4 %reduce-scatter.3.cloned.1.call-done = bf16[64,6144]{1,0:T(8,128)(2,1)} async-done(((bf16[1024,6144]{1,0:T(8,128)(2,1)}), bf16[64,6144]{1,0:T(8,128)(2,1)}) %reduce-scatter.3.cloned.1.call-update) | async-done | bytes 786448 | tf_op jit(solution)/shard_map/reduce_scatter | solution.py:93
  453.4 3.1 fusion.73
  (148 shorter events, 64.2 us)
Async XLA Ops:
  7.2 5.3 %copy-start.6 = (s32[1024]{0:T(1024)S(1)}, s32[1024]{0:T(1024)}, u32[]{:S(2)}) copy-start(s32[1024]{0:T(1024)} %param.14) | copy-start | bytes 12292
  7.2 81.8 %all-gather.3.cloned.1.call-start = ((), (), s32[]{:S(2)}) async-start(), calls=%async_computation.2 | async-start | bytes 13369344 | tf_op jit(solution)/shard_map/all_gather | solution.py:85
  8.7 0.6 copy-start.7
  11.6 149.9 %all-gather.5.cloned.1.call-start = ((), (), s32[]{:S(2)}) async-start(), calls=%async_computation.4 | async-start | bytes 13369344 | tf_op jit(solution)/shard_map/all_gather | solution.py:95
  12.4 363.5 %reduce-scatter.5.cloned.1.call-start = ((), (), s32[]{:S(2)}) async-start(), calls=%async_computation.5 | async-start | bytes 13369344 | tf_op jit(solution)/shard_map/reduce_scatter | solution.py:104
  193.6 9.3 %copy-start.4 = (bf16[1024,128]{1,0:T(8,128)(2,1)S(1)}, bf16[1024,128]{1,0:T(8,128)(2,1)}, u32[]{:S(2)}) copy-start(bf16[1024,128]{1,0:T(8,128)(2,1)} %custom-call) | copy-start | bytes 786436
  249.3 2.0 copy-start.1
  249.3 2.0 copy-start.2
  301.2 152.3 %reduce-scatter.3.cloned.1.call-start = ((), (), s32[]{:S(2)}) async-start(), calls=%async_computation.3 | async-start | bytes 13369344 | tf_op jit(solution)/shard_map/reduce_scatter | solution.py:93
  344.1 27.7 %collective-permute-start.1 = (f32[6144,128]{1,0:T(8,128)S(1)}, f32[6144,128]{1,0:T(8,128)S(1)}, u32[]{:S(2)}, u32[]{:S(2)}) collective-permute-start(f32[6144,128]{1,0:T(8,128)S(1)} %fusion.128), channel_id=1, source_target_pairs={{0,1},{1,0},{2,3},{3,2},{4,5},{5,4},{6,7},{7,6},{8,9},{9,8},{10,11... | collective-permute-start | bytes 9437192 | tf_op jit(solution)/shard_map/ppermute | solution.py:67
  344.5 18.8 %slice-start = ((s8[12582912]{0:T(1024)(128)(4,1)}), s8[4194304]{0:T(1024)(128)(4,1)S(1)}, s32[]{:S(2)}) async-start(s8[12582912]{0:T(1024)(128)(4,1)} %bitcast.225), calls=%async_computation.6 | async-start | bytes 8388608
  344.5 18.8 %slice-start.1 = ((s8[12582912]{0:T(1024)(128)(4,1)}), s8[4194304]{0:T(1024)(128)(4,1)S(1)}, s32[]{:S(2)}) async-start(s8[12582912]{0:T(1024)(128)(4,1)} %bitcast.225), calls=%async_computation.7 | async-start | bytes 8388608
  351.2 12.1 %slice-start.2 = ((s8[12582912]{0:T(1024)(128)(4,1)}), s8[4194304]{0:T(1024)(128)(4,1)S(1)}, s32[]{:S(2)}) async-start(s8[12582912]{0:T(1024)(128)(4,1)} %bitcast.225), calls=%async_computation.8 | async-start | bytes 8388608
  351.2 22.6 %collective-permute-start = (f32[6144,128]{1,0:T(8,128)S(1)}, f32[6144,128]{1,0:T(8,128)S(1)}, u32[]{:S(2)}, u32[]{:S(2)}) collective-permute-start(f32[6144,128]{1,0:T(8,128)S(1)} %fusion.110), channel_id=1, source_target_pairs={{0,1},{1,0},{2,3},{3,2},{4,5},{5,4},{6,7},{7,6},{8,9},{9,8},{10,11... | collective-permute-start | bytes 9437192 | tf_op jit(solution)/shard_map/ppermute | solution.py:67
  373.9 2.0 copy-start
  373.9 2.0 copy-start.5
  373.9 2.0 copy-start.8
  373.9 79.6 %copy-start.3 = (bf16[64,6144]{1,0:T(8,128)(2,1)S(1)}, bf16[64,6144]{1,0:T(8,128)(2,1)}, u32[]{:S(2)}) copy-start(bf16[64,6144]{1,0:T(8,128)(2,1)} %param.13) | copy-start | bytes 2359300
Sparse Core Ops, SparseCore 0:
  11.7 77.2 all-gather.2
  90.6 70.7 all-gather.4
  301.3 73.6 reduce-scatter.4
  377.2 76.2 reduce-scatter.2
where the time goes:
time: 468 us; the launch traced here: 463 us
  matrix products  185 us (40%)
  waiting for transfers between devices  168 us (36%)
  blocking collectives  44.4 us (9%)
  other arithmetic  33.1 us (7%)
  local copies, waits for them, and re-layouts  16.5 us (4%)
  between operations  14.4 us (3%)
    all_gather x1, waiting for transfers between devices, device_step(): h_full = lax.all_gather(hidden, 'tp', axis=0, tiled=True)  76.4 us
    all_gather x1, waiting for transfers between devices, device_step(): dy_full = lax.all_gather(dy_blk, 'tp', axis=0, tiled=True)  59.6 us
    psum x1, blocking collectives, device_step(): d_gain = lax.psum(dg_part, 'tp')  44.4 us
    reduce_scatter x1, waiting for transfers between devices, device_step(): mix_rows = lax.psum_scatter(mix_part, 'tp', scatter_dimension=0, tiled=True)  31.4 us
    dot_general x12, matrix products, one_block(): jnp.einsum('hqs,sd->qhd', prob_blk, v_raw, preferred_element_type=jnp.flo...  31.3 us
    dot_general x1, matrix products, device_step(): lax.dot_general(dq_flat, wq_loc, contract_cols, preferred_element_type=jn...  23.6 us
    dot_general x1, matrix products, device_step(): lax.dot_general(d_v, wv_loc, contract_cols, preferred_element_type=jnp.fl...  13.2 us
    dot_general x1, matrix products, device_step(): jnp.dot(o_flat, wo_loc, preferred_element_type=jnp.float32)  12 us
  transfers between devices with their start and end apart: 6, of which 3 were waited for; matrix products, arithmetic and copies ran while one was open for 19% of the time, Pallas kernels for 0%

commit v1 on v0

v1 whole, which is shorter than its diff:
```python
import functools
import jax
import jax.numpy as jnp
from jax import lax
from jax.experimental import pallas as pl
from jax.experimental.pallas import tpu as pltpu
from jax.sharding import PartitionSpec as P

HEAD_DIM = 128
TILE = 128
SUBS = 4
SCORE_SCALE = HEAD_DIM ** -0.5
ROPE_THETA = 1000000.0
NORM_EPS = 1e-05
MASKED = -1e30
MESH = pl.DeviceIdType.MESH
F32 = jnp.float32
BF16 = jnp.bfloat16
ANY = pl.BlockSpec(memory_space=pl.ANY)
VM = pl.BlockSpec(memory_space=pltpu.VMEM)
NT = (((1,), (1,)), ((), ()))
TN = (((0,), (0,)), ((), ()))
VMEM_LIMIT = 63 * 1024 * 1024


def dot(a, b, dims=(((1,), (0,)), ((), ()))):
    return lax.dot_general(a, b, dims, preferred_element_type=F32)


class Ring:
    def __init__(self, tp):
        self.tp = tp
        self.nz = tp // 2
        self.me = lax.axis_index("tp")
        self.c = self.me // 2
        self.k = self.me % 2
        self.up = lax.rem(self.c + 1, self.nz) * 2 + self.k
        self.dn = lax.rem(self.c + self.nz - 1, self.nz) * 2 + self.k
        self.pt = self.c * 2 + 1 - self.k

    def barrier(self):
        bar = pltpu.get_barrier_semaphore()
        for d in (self.up, self.dn, self.pt):
            pl.semaphore_signal(bar, inc=1, device_id={"tp": d}, device_id_type=MESH)
        pl.semaphore_wait(bar, 3)

    def barrier_all(self):
        bar = pltpu.get_barrier_semaphore()
        for o in range(1, self.tp):
            pl.semaphore_signal(bar, inc=1, device_id={"tp": lax.rem(self.me + o, self.tp)}, device_id_type=MESH)
        pl.semaphore_wait(bar, self.tp - 1)

    def chip(self, n):
        return lax.rem(n + 2 * self.nz, self.nz)


def remote(src, dst, ss, rs, dev):
    return pltpu.make_async_remote_copy(src, dst, ss, rs, device_id={"tp": dev}, device_id_type=MESH)


class Gather:
    def __init__(self, rg, src, dst, rows, ss, rs, dss, drs, ls):
        self.rg, self.src, self.dst, self.R = rg, src, dst, rows
        self.ss, self.rs, self.dss, self.drs, self.ls = ss, rs, dss, drs, ls
        self.H = rows // 2
        self.steps = rg.nz - 1

    def rows(self, chip, core, half):
        return pl.ds(pl.multiple_of((self.rg.chip(chip) * 2 + core) * self.R + half * self.H, self.H), self.H)

    def half(self, d, s):
        return s % 2 if d == 0 else 1 - s % 2

    def origin(self, d, s):
        h = (s + 2) // 2
        return self.rg.c - h if d == 0 else self.rg.c + h

    def dev(self, d):
        return self.rg.up if d == 0 else self.rg.dn

    def own(self, d, s):
        h = self.half(d, s)
        return remote(self.src.at[pl.ds(h * self.H, self.H), :], self.dst.at[self.rows(self.rg.c, self.rg.k, h), :],
                      self.ss.at[d, s], self.rs.at[d, s], self.dev(d))

    def recv_rows(self, d, s, core):
        return self.rows(self.origin(d, s), core, self.half(d, s))

    def fwd(self, d, s):
        r = self.recv_rows(d, s - 2, self.rg.k)
        return remote(self.dst.at[r, :], self.dst.at[r, :], self.ss.at[d, s], self.rs.at[d, s], self.dev(d))

    def recv(self, d, s):
        r = self.recv_rows(d, s, self.rg.k)
        return remote(self.dst.at[r, :], self.dst.at[r, :], self.ss.at[d, s], self.rs.at[d, s], self.dev(d))

    def pair(self, i, r):
        return remote(self.dst.at[r, :], self.dst.at[r, :], self.dss.at[i], self.drs.at[i], self.rg.pt)

    def block(self, dev):
        return pl.ds(pl.multiple_of(dev * self.R, self.R), self.R)

    def pair_own(self):
        return remote(self.src, self.dst.at[self.block(self.rg.me), :], self.dss.at[0], self.drs.at[0], self.rg.pt)

    def local(self):
        return pltpu.make_async_copy(self.src, self.dst.at[self.block(self.rg.me), :], self.ls)

    def start_ring(self, s):
        for d in range(2):
            self.own(d, s).start()

    def start_local(self):
        self.local().start()
        self.pair_own().start()

    def tick(self, s, forward=True):
        for d in range(2):
            self.recv(d, s).wait_recv()
            if isinstance(s, int):
                if s + 2 < self.steps:
                    self.fwd(d, s + 2).start()
            else:
                @pl.when(s + 2 < self.steps)
                def _():
                    self.fwd(d, s + 2).start()
            self.pair(1 + 2 * s + d, self.recv_rows(d, s, self.rg.k)).start()

    def wait_pair(self):
        self.local().wait()
        self.pair(0, self.block(self.rg.pt)).wait_recv()
        for s in range(self.steps):
            for d in range(2):
                self.pair(1 + 2 * s + d, self.recv_rows(d, s, 1 - self.rg.k)).wait_recv()

    def drain(self):
        self.pair_own().wait_send()
        for s in range(self.steps):
            for d in range(2):
                self.pair(1 + 2 * s + d, self.recv_rows(d, s, self.rg.k)).wait_send()
                if s < 2:
                    self.own(d, s).wait_send()
                else:
                    self.fwd(d, s).wait_send()

    @staticmethod
    def scratch(tp):
        n = tp // 2 - 1
        dma = pltpu.SemaphoreType.DMA
        return [dma((2, n)), dma((2, n)), dma((1 + 2 * n,)), dma((1 + 2 * n,)), dma]


class Scatter:
    def __init__(self, rg, own, peer, pre, psem, buf, ss, rs, final):
        self.rg, self.own, self.peer, self.pre, self.psem = rg, own, peer, pre, psem
        self.buf, self.ss, self.rs, self.final = buf, ss, rs, final
        self.W = pre.shape[-1]
        self.CW = self.W // SUBS

    def blk(self, d, s):
        return self.rg.chip(self.rg.c - 1 - s) if d == 0 else self.rg.chip(self.rg.c + 1 + s)

    def load(self, w, d, s):
        src = (self.own, self.peer)[w].at[self.blk(d, s), :, pl.ds(d * self.W, self.W)]
        return pltpu.make_async_copy(src, self.pre.at[s % 2, w, d], self.psem.at[s % 2, w, d])

    def loads(self, s):
        return [self.load(w, d, s) for w in range(2) for d in range(2)]

    def send(self, d, u, s):
        return remote(self.buf.at[d, u, s], self.buf.at[d, u, s + 1], self.ss.at[d, u, s], self.rs.at[d, u, s],
                      self.rg.up if d == 0 else self.rg.dn)

    def tick(self, s, u):
        nz = self.rg.nz
        if u == 0:
            for cp in self.loads(s):
                cp.wait()

            @pl.when(s + 1 < nz)
            def _():
                for cp in self.loads(s + 1):
                    cp.start()
        cols = slice(u * self.CW, (u + 1) * self.CW)
        slot = s % 2

        def mine(d):
            return self.pre[slot, 0, d, :, cols].astype(F32) + self.pre[slot, 1, d, :, cols].astype(F32)

        for d in range(2):
            @pl.when(s == 0)
            def _():
                self.buf[d, u, s] = mine(d).astype(BF16)
                self.send(d, u, s).start()

            @pl.when((s > 0) & (s < nz - 1))
            def _():
                self.send(d, u, s - 1).wait_recv()
                self.buf[d, u, s] = (mine(d) + self.buf[d, u, s].astype(F32)).astype(BF16)
                self.send(d, u, s).start()

            @pl.when(s == nz - 1)
            def _():
                self.send(d, u, s - 1).wait_recv()
                self.final(d, u, mine(d) + self.buf[d, u, s].astype(F32))

    def drain(self):
        @pl.loop(0, self.rg.nz - 1)
        def _(s):
            for d in range(2):
                for u in range(SUBS):
                    self.send(d, u, s).wait_send()

    @staticmethod
    def scratch(tp, rows, d_model):
        nz = tp // 2
        dma = pltpu.SemaphoreType.DMA
        W = d_model // 2
        return [pltpu.VMEM((2, 2, 2, rows, W), BF16), dma((2, 2, 2)), pltpu.VMEM((2, SUBS, nz, rows, W // SUBS), BF16),
                dma((2, SUBS, nz - 1)), dma((2, SUBS, nz - 1))]


def weight_copies(kv, wq, wk, wv, wo, w_all, wo_v, sem):
    dq = wq.shape[1]
    kvc = pl.ds(pl.multiple_of(kv * HEAD_DIM, HEAD_DIM), HEAD_DIM)
    return [pltpu.make_async_copy(wq, w_all.at[:, pl.ds(0, dq)], sem.at[0]),
            pltpu.make_async_copy(wk.at[:, kvc], w_all.at[:, pl.ds(dq, HEAD_DIM)], sem.at[1]),
            pltpu.make_async_copy(wv.at[:, kvc], w_all.at[:, pl.ds(dq + HEAD_DIM, HEAD_DIM)], sem.at[2]),
            pltpu.make_async_copy(wo, wo_v, sem.at[3])]


def rope(t, cos, sin):
    return t * cos + pltpu.roll(t, HEAD_DIM // 2, 1) * sin


def rope_t(t, cos, sin):
    return t * cos - pltpu.roll(t, HEAD_DIM // 2, 1) * sin


def to_col(row):
    return jnp.broadcast_to(row, (TILE, TILE)).T


def trow(i, n=TILE):
    return pl.ds(pl.multiple_of(i * n, n), n)


def keep_t(kdc, kdr, i, seq):
    key = lax.broadcasted_iota(jnp.int32, (seq, TILE), 0)
    qry = lax.broadcasted_iota(jnp.int32, (seq, TILE), 1) + i * TILE
    return (key <= qry) & (kdc == kdr)


def fwd_kernel(tp, kvr, x_ref, g_ref, pos_ref, frq_ref, dy_ref, wq, wk, wv, wo,
               h_full, dy_full, mix_own, mix_peer, q3_ref, k_ref, v_ref, ot_ref, st_ref, cos_ref, sin_ref, kdc_ref, kdr_ref,
               hown, w_all, wo_v, htile, stage, vt, wsem, hsem, osem, pss, prs, *gsem):
    rg = Ring(tp)
    rows, dm = x_ref.shape
    seq = rows * tp
    nt = seq // TILE
    nh = wq.shape[1] // HEAD_DIM
    half = TILE // 2
    ga = Gather(rg, hown, h_full, rows, *gsem[:5])
    gd = Gather(rg, dy_ref, dy_full, rows, *gsem[5:])
    wcp = weight_copies(rg.me // kvr, wq, wk, wv, wo, w_all, wo_v, wsem)
    for cp in wcp:
        cp.start()
    RB = 16

    @pl.loop(0, rows // RB)
    def _(r):
        xf = x_ref[trow(r, RB), :].astype(F32)
        inv = lax.rsqrt(jnp.mean(xf * xf, axis=-1, keepdims=True) + NORM_EPS)
        hown[trow(r, RB), :] = (xf * inv * g_ref[...]).astype(BF16)

    rg.barrier()
    ga.start_ring(0)
    ga.start_ring(1)
    ga.start_local()
    gd.start_local()
    lane = lax.broadcasted_iota(jnp.int32, (TILE, TILE), 1)
    sgn = jnp.where(lane < HEAD_DIM // 2, -1.0, 1.0).astype(F32)

    kdr_ref[...] = pos_ref[...] - (lax.broadcasted_iota(jnp.int32, pos_ref.shape, 0) * TILE
                                   + lax.broadcasted_iota(jnp.int32, pos_ref.shape, 1)).astype(F32)

    @pl.loop(0, nt)
    def _(i):
        ang = to_col(pos_ref[pl.ds(i, 1), :]) * frq_ref[...]
        cos_ref[trow(i), :] = jnp.cos(ang)
        sin_ref[trow(i), :] = jnp.sin(ang) * sgn
        kdc_ref[trow(i), :] = to_col(kdr_ref[pl.ds(i, 1), :])

    for s in range(ga.steps):
        ga.tick(s)
        if s >= ga.steps - 2:
            gd.start_ring(s - (ga.steps - 2))
    ga.wait_pair()
    for cp in wcp:
        cp.wait()

    def hload(i):
        return pltpu.make_async_copy(h_full.at[trow(i), :], htile.at[i % 2], hsem.at[i % 2])

    hload(0).start()

    @pl.loop(0, nt)
    def _(i):
        hload(i).wait()

        @pl.when(i + 1 < nt)
        def _():
            hload(i + 1).start()
        qkv = dot(htile[i % 2], w_all[...])
        cos, sin = cos_ref[trow(i), :], sin_ref[trow(i), :]
        for h in range(nh + 1):
            t = qkv[:, h * HEAD_DIM:(h + 1) * HEAD_DIM].astype(BF16).astype(F32)
            t = rope(t, cos, sin).astype(BF16)
            if h < nh:
                q3_ref[i, pl.ds(h * TILE, TILE), :] = t
            else:
                k_ref[trow(i), :] = t
        v = qkv[:, (nh + 1) * HEAD_DIM:].astype(BF16)
        v_ref[trow(i), :] = v
        vt[:, trow(i)] = v.astype(F32).T.astype(BF16)

    def outs(i):
        sl = i % 2
        mine = stage.at[sl, trow(rg.k, half), :]
        other = stage.at[sl, trow(1 - rg.k, half), :]
        return (pltpu.make_async_copy(mine, mix_own.at[i], osem.at[sl]),
                remote(other, mix_peer.at[i], pss.at[i], prs.at[i], rg.pt))

    @pl.loop(0, nt)
    def _(i):
        @pl.when(i < gd.steps)
        def _():
            gd.tick(i)

        s = dot(k_ref[...], q3_ref[i], NT) * SCORE_SCALE
        keep = keep_t(kdc_ref[...], kdr_ref[pl.ds(i, 1), :], i, seq)
        pbs = []
        for h in range(nh):
            sh = jnp.where(keep, s[:, h * TILE:(h + 1) * TILE], MASKED)
            m = jnp.max(sh, axis=0, keepdims=True)
            e = jnp.exp(sh - m)
            li = 1.0 / jnp.sum(e, axis=0, keepdims=True)
            st_ref[i, pl.ds(0, 1), pl.ds(h * TILE, TILE)] = m
            st_ref[i, pl.ds(1, 1), pl.ds(h * TILE, TILE)] = li
            pbs.append((e * li).astype(BF16))
        ot = dot(vt[...], jnp.concatenate(pbs, axis=1))
        os = []
        for h in range(nh):
            oh = ot[:, h * TILE:(h + 1) * TILE]
            ot_ref[pl.ds(h * HEAD_DIM, HEAD_DIM), trow(i)] = oh.astype(BF16)
            os.append(oh.T.astype(BF16))
        o = jnp.concatenate(os, axis=1)

        @pl.when(i >= 2)
        def _():
            a, b = outs(i - 2)
            a.wait()
            b.wait_send()
        NC = dm // 4
        for n in range(4):
            stage[i % 2, :, pl.ds(n * NC, NC)] = dot(o, wo_v[:, pl.ds(n * NC, NC)]).astype(BF16)
        a, b = outs(i)
        a.start()
        b.start()

    for i in (nt - 2, nt - 1):
        a, b = outs(i)
        a.wait()
        b.wait_send()
    for i in range(nt):
        outs(i)[1].wait_recv()
    gd.wait_pair()
    ga.drain()
    gd.drain()


def bwd_kernel(tp, kvr, mix_own, mix_peer, x_ref, dy_full, wq, wk, wv, wo, q3_ref, k_ref, v_ref, st_ref, cos_ref, sin_ref, kdc_ref, kdr_ref,
               out_ref, dqkv_ref, dh_own, dh_peer,
               w_all, wo_v, dyt, stage, kt, dk_acc, dv_acc, do3, dqkv_t, wsem, ysem, osem, pss, prs, *rsem):
    rg = Ring(tp)
    rows, dm = x_ref.shape
    seq = rows * tp
    nt = seq // TILE
    np_ = nt // 2
    nh = wq.shape[1] // HEAD_DIM
    dq = wq.shape[1]
    half = TILE // 2

    def final(d, u, val):
        cs = pl.ds(d * sc.W + u * sc.CW, sc.CW)
        out_ref[:, cs] = (x_ref[:, cs].astype(F32) + val).astype(BF16)

    sc = Scatter(rg, mix_own, mix_peer, *rsem, final)
    for cp in sc.loads(0):
        cp.start()
    wcp = weight_copies(rg.me // kvr, wq, wk, wv, wo, w_all, wo_v, wsem)

    def yload(it):
        return pltpu.make_async_copy(dy_full.at[trow(np_ - 1 - it, 2 * TILE), :], dyt.at[it % 2], ysem.at[it % 2])

    yload(0).start()
    for cp in (wcp[3], wcp[0], wcp[1], wcp[2]):
        cp.start()
    rg.barrier()
    for u in range(SUBS):
        sc.tick(0, u)
    kt[...] = k_ref[...].astype(F32).T.astype(BF16)
    dk_acc[...] = jnp.zeros_like(dk_acc)
    dv_acc[...] = jnp.zeros_like(dv_acc)
    for cp in wcp:
        cp.wait()

    def outs(i, sl, j):
        mine = stage.at[sl, pl.ds(pl.multiple_of(j * TILE + rg.k * half, half), half), :]
        other = stage.at[sl, pl.ds(pl.multiple_of(j * TILE + (1 - rg.k) * half, half), half), :]
        return (pltpu.make_async_copy(mine, dh_own.at[i], osem.at[sl, j]),
                remote(other, dh_peer.at[i], pss.at[i], prs.at[i], rg.pt))

    def attn(i, j):
        q3 = q3_ref[i]
        do = do3[j]
        s = dot(k_ref[...], q3, NT) * SCORE_SCALE
        keep = keep_t(kdc_ref[...], kdr_ref[pl.ds(i, 1), :], i, seq)
        dp = dot(v_ref[...], do, NT)
        pbs, dss = [], []
        for h in range(nh):
            hs = slice(h * TILE, (h + 1) * TILE)
            m = st_ref[i, pl.ds(0, 1), pl.ds(h * TILE, TILE)]
            li = st_ref[i, pl.ds(1, 1), pl.ds(h * TILE, TILE)]
            p = jnp.exp(jnp.where(keep, s[:, hs], MASKED) - m) * li
            dph = dp[:, hs].astype(BF16).astype(F32)
            dl = jnp.sum(dph * p, axis=0, keepdims=True)
            dss.append((p * (dph - dl) * SCORE_SCALE).astype(BF16))
            pbs.append(p.astype(BF16))
        pb = jnp.concatenate(pbs, axis=1)
        ds = jnp.concatenate(dss, axis=1)
        dv_acc[...] += dot(pb, do)
        dk_acc[...] += dot(ds, q3)
        dqt = dot(kt[...], ds)
        cos, sin = cos_ref[trow(i), :], sin_ref[trow(i), :]
        jr = pl.ds(j * TILE, TILE)
        for h in range(nh):
            t = dqt[:, h * TILE:(h + 1) * TILE].T.astype(BF16).astype(F32)
            dqkv_t[jr, pl.ds(h * HEAD_DIM, HEAD_DIM)] = rope_t(t, cos, sin).astype(BF16)
        t = dk_acc[trow(i), :].astype(BF16).astype(F32)
        dqkv_t[jr, pl.ds(dq, HEAD_DIM)] = rope_t(t, cos, sin).astype(BF16)
        dqkv_t[jr, pl.ds(dq + HEAD_DIM, HEAD_DIM)] = dv_acc[trow(i), :].astype(BF16)

    @pl.loop(0, np_)
    def _(it):
        ip = np_ - 1 - it
        sl = it % 2
        yload(it).wait()

        @pl.when(it + 1 < np_)
        def _():
            yload(it + 1).start()

        def tick(j, u):
            s = 2 * it + j
            if j == 0:
                @pl.when(s > 0)
                def _():
                    sc.tick(s, u)
            else:
                sc.tick(s, u)

        tick(0, 0)
        do = dot(dyt[sl], wo_v[...], NT).astype(BF16)
        for j in range(2):
            for h in range(nh):
                do3[j, pl.ds(h * TILE, TILE), :] = do[j * TILE:(j + 1) * TILE, h * HEAD_DIM:(h + 1) * HEAD_DIM]
        tick(0, 1)
        attn(2 * ip + 1, 1)
        tick(0, 2)
        attn(2 * ip, 0)
        tick(0, 3)
        dqkv_ref[trow(ip, 2 * TILE), :] = dqkv_t[...]

        @pl.when(it >= 2)
        def _():
            for j in range(2):
                a, b = outs(2 * (ip + 2) + j, sl, j)
                a.wait()
                b.wait_send()
        NC = dm // 4
        for n in range(4):
            ns = pl.ds(n * NC, NC)
            stage[sl, :, ns] = dot(dqkv_t[...], w_all[ns, :], NT).astype(BF16)
            tick(1, n)
        for j in range(2):
            a, b = outs(2 * ip + j, sl, j)
            a.start()
            b.start()

    for it in (np_ - 2, np_ - 1):
        ip = np_ - 1 - it
        for j in range(2):
            a, b = outs(2 * ip + j, it % 2, j)
            a.wait()
            b.wait_send()
    for i in range(nt):
        outs(i, 0, 0)[1].wait_recv()
    sc.drain()


def grad_kernel(tp, dh_own, dh_peer, x_ref, dy_ref, g_ref, h_full, dy_full, dqkv_ref, ot_ref,
                gx_ref, dg_ref, dwq, dwk, dwv, dwo,
                ht, yt, sq, skv, so, peer, dhr, part, slots, tot, hsem, ysem, osem, pss, prs, gss, grs, bss, brs, *rsem):
    rg = Ring(tp)
    rows, dm = x_ref.shape
    nz = rg.nz
    dq = dwq.shape[1]
    CB = dm // nz

    def final(d, u, val):
        dhr[:, pl.ds(d * sc.W + u * sc.CW, sc.CW)] = val.astype(BF16)

    sc = Scatter(rg, dh_own, dh_peer, *rsem, final)
    for cp in sc.loads(0):
        cp.start()

    def col(it):
        return pl.ds(pl.multiple_of(it * CB, CB), CB)

    def hload(it):
        return pltpu.make_async_copy(h_full.at[:, col(it)], ht.at[it % 2], hsem.at[it % 2])

    def yload(it):
        return pltpu.make_async_copy(dy_full.at[:, col(it)], yt.at[it % 2], ysem.at[it % 2])

    hload(0).start()
    yload(0).start()
    rg.barrier_all()

    def to_peer(it):
        return remote(skv.at[it % 2], peer.at[it], pss.at[it], prs.at[it], rg.pt)

    def outs(it):
        sl = it % 2
        return [pltpu.make_async_copy(sq.at[sl], dwq.at[col(it), :], osem.at[sl, 0]),
                pltpu.make_async_copy(so.at[sl], dwo.at[:, col(it)], osem.at[sl, 1])]

    def kv_outs(it):
        return [pltpu.make_async_copy(peer.at[it, :, pl.ds(0, HEAD_DIM)], dwk.at[col(it), :], osem.at[it % 2, 2]),
                pltpu.make_async_copy(peer.at[it, :, pl.ds(HEAD_DIM, HEAD_DIM)], dwv.at[col(it), :], osem.at[it % 2, 3])]

    def pair_sum(it):
        to_peer(it).wait_recv()
        peer[it] = peer[it] + skv[it % 2]
        to_peer(it).wait_send()
        for cp in kv_outs(it):
            cp.start()

    HC = CB // 2

    @pl.loop(0, nz)
    def _(it):
        sl = it % 2
        hload(it).wait()
        yload(it).wait()

        @pl.when(it + 1 < nz)
        def _():
            hload(it + 1).start()
            yload(it + 1).start()

        @pl.when(it >= 2)
        def _():
            for cp in outs(it - 2) + kv_outs(it - 2):
                cp.wait()
        for n in range(2):
            sc.tick(it, 2 * n)
            hs = pl.ds(n * HC, HC)
            dw = dot(ht[sl, :, hs], dqkv_ref[...], TN)
            sq[sl, hs, :] = dw[:, :dq].astype(BF16)
            skv[sl, hs, :] = dw[:, dq:]
            sc.tick(it, 2 * n + 1)
            so[sl, :, hs] = dot(ot_ref[...], yt[sl, :, hs]).astype(BF16)
        to_peer(it).start()
        for cp in outs(it):
            cp.start()

        @pl.when(it >= 1)
        def _():
            pair_sum(it - 1)

    pair_sum(nz - 1)
    RB = 16
    part[...] = jnp.zeros_like(part)

    @pl.loop(0, rows // RB)
    def _(r):
        rr = trow(r, RB)
        xf = x_ref[rr, :].astype(F32)
        inv = lax.rsqrt(jnp.mean(xf * xf, axis=-1, keepdims=True) + NORM_EPS)
        xh = xf * inv
        dh = dhr[rr, :].astype(F32)
        part[...] += jnp.sum(dh * xh, axis=0, keepdims=True)
        a = dh * g_ref[...]
        di = inv * (a - xh * jnp.mean(a * xh, axis=-1, keepdims=True))
        gx_ref[rr, :] = (dy_ref[rr, :].astype(F32) + di).astype(BF16)

    GW = dm // tp

    def gcol(dev):
        return pl.ds(pl.multiple_of(dev * GW, GW), GW)

    def dev(o):
        return lax.rem(rg.me + o, tp)

    def scat(o):
        return remote(part.at[:, gcol(dev(o))], slots.at[o], gss.at[o], grs.at[o], dev(o))

    for o in range(1, tp):
        scat(o).start()
    acc = part[:, gcol(rg.me)]
    for o in range(1, tp):
        scat(o).wait_recv()
        acc = acc + slots[o]
    tot[...] = acc

    def bcast(o):
        return remote(tot, dg_ref.at[:, gcol(rg.me)], bss.at[o], brs.at[o], dev(o))

    def arrive(o):
        src = lax.rem(rg.me + tp - o, tp)
        return remote(tot, dg_ref.at[:, gcol(src)], bss.at[o], brs.at[o], dev(o))

    for o in range(1, tp):
        bcast(o).start()
    dg_ref[:, gcol(rg.me)] = acc
    for o in range(1, tp):
        arrive(o).wait_recv()
    for o in range(1, tp):
        scat(o).wait_send()
        bcast(o).wait_send()
    for it in (nz - 2, nz - 1):
        for cp in outs(it) + kv_outs(it):
            cp.wait()
    sc.drain()


def solution(mesh):
    tp = mesh.shape["tp"]
    nz = tp // 2
    DMA = pltpu.SemaphoreType.DMA

    def device_step(x, dy, pos, gain, wq, wk, wv, wo):
        rows, dm = x.shape
        seq = rows * tp
        nt = seq // TILE
        dq = wq.shape[1]
        nh = dq // HEAD_DIM
        qr = nh * TILE
        wd = dq + 2 * HEAD_DIM
        kvr = tp // (wk.shape[1] // HEAD_DIM)
        expo = jnp.arange(0, HEAD_DIM, 2, dtype=F32) / HEAD_DIM
        frq = jnp.power(ROPE_THETA, -expo)
        frq = jnp.concatenate([frq, frq]).reshape(1, HEAD_DIM)
        g2 = gain.reshape(1, dm)
        posf = pos.astype(F32).reshape(nt, TILE)

        def sds(shape, dt):
            return jax.ShapeDtypeStruct(shape, dt)

        full = sds((seq, dm), BF16)
        blocks = sds((nt, rows, dm), BF16)
        (h_full, dy_full, mix_own, mix_peer, q3, kk, vv, ot, st, cos, sin, kdc, kdr) = pl.pallas_call(
            functools.partial(fwd_kernel, tp, kvr),
            out_shape=[full, full, blocks, blocks, sds((nt, qr, HEAD_DIM), BF16), sds((seq, HEAD_DIM), BF16), sds((seq, HEAD_DIM), BF16),
                       sds((dq, seq), BF16), sds((nt, 2, qr), F32), sds((seq, HEAD_DIM), F32), sds((seq, HEAD_DIM), F32),
                       sds((seq, TILE), F32), sds((nt, TILE), F32)],
            in_specs=[VM, VM, VM, VM, ANY, ANY, ANY, ANY, ANY],
            out_specs=[ANY] * 4 + [VM] * 9,
            scratch_shapes=[pltpu.VMEM((rows, dm), BF16), pltpu.VMEM((dm, wd), BF16), pltpu.VMEM((dq, dm), BF16),
                            pltpu.VMEM((2, TILE, dm), BF16), pltpu.VMEM((2, TILE, dm), BF16), pltpu.VMEM((HEAD_DIM, seq), BF16),
                            DMA((4,)), DMA((2,)), DMA((2,)), DMA((nt,)), DMA((nt,))] + Gather.scratch(tp) + Gather.scratch(tp),
            compiler_params=pltpu.CompilerParams(collective_id=1, has_side_effects=True, vmem_limit_bytes=VMEM_LIMIT),
            name="gather_fwd",
        )(x, g2, posf, frq, dy, wq, wk, wv, wo)

        out, dqkv, dh_own, dh_peer = pl.pallas_call(
            functools.partial(bwd_kernel, tp, kvr),
            out_shape=[sds((rows, dm), BF16), sds((seq, wd), BF16), blocks, blocks],
            in_specs=[ANY, ANY, VM, ANY, ANY, ANY, ANY, ANY] + [VM] * 8,
            out_specs=[VM, VM, ANY, ANY],
            scratch_shapes=[pltpu.VMEM((dm, wd), BF16), pltpu.VMEM((dq, dm), BF16), pltpu.VMEM((2, 2 * TILE, dm), BF16),
                            pltpu.VMEM((2, 2 * TILE, dm), BF16), pltpu.VMEM((HEAD_DIM, seq), BF16), pltpu.VMEM((seq, HEAD_DIM), F32),
                            pltpu.VMEM((seq, HEAD_DIM), F32), pltpu.VMEM((2, qr, HEAD_DIM), BF16), pltpu.VMEM((2 * TILE, wd), BF16),
                            DMA((4,)), DMA((2,)), DMA((2, 2)), DMA((nt,)), DMA((nt,))] + Scatter.scratch(tp, rows, dm),
            compiler_params=pltpu.CompilerParams(collective_id=2, has_side_effects=True, vmem_limit_bytes=VMEM_LIMIT),
            name="scatter_bwd",
        )(mix_own, mix_peer, x, dy_full, wq, wk, wv, wo, q3, kk, vv, st, cos, sin, kdc, kdr)

        CB = dm // nz
        grad_x, d_gain, d_wq, d_wk, d_wv, d_wo = pl.pallas_call(
            functools.partial(grad_kernel, tp),
            out_shape=[sds((rows, dm), BF16), sds((1, dm), F32), sds((dm, dq), BF16), sds((dm, HEAD_DIM), F32), sds((dm, HEAD_DIM), F32),
                       sds((dq, dm), BF16)],
            in_specs=[ANY, ANY, VM, VM, VM, ANY, ANY, VM, VM],
            out_specs=[VM, VM, ANY, ANY, ANY, ANY],
            scratch_shapes=[pltpu.VMEM((2, seq, CB), BF16), pltpu.VMEM((2, seq, CB), BF16), pltpu.VMEM((2, CB, dq), BF16),
                            pltpu.VMEM((2, CB, 2 * HEAD_DIM), F32), pltpu.VMEM((2, dq, CB), BF16), pltpu.VMEM((nz, CB, 2 * HEAD_DIM), F32),
                            pltpu.VMEM((rows, dm), BF16), pltpu.VMEM((1, dm), F32), pltpu.VMEM((tp, 1, dm // tp), F32), pltpu.VMEM((1, dm // tp), F32),
                            DMA((2,)), DMA((2,)), DMA((2, 4)), DMA((nz,)), DMA((nz,)), DMA((tp,)), DMA((tp,)), DMA((tp,)), DMA((tp,))]
            + Scatter.scratch(tp, rows, dm),
            compiler_params=pltpu.CompilerParams(collective_id=3, has_side_effects=True, vmem_limit_bytes=VMEM_LIMIT),
            name="scatter_grads",
        )(dh_own, dh_peer, x, dy, g2, h_full, dy_full, dqkv, ot)
        return out, grad_x, d_wq, d_wk, d_wv, d_wo, d_gain.reshape(dm)

    specs_in = (P(('dp', 'tp'), None), P(('dp', 'tp'), None), P('dp'), P(), P(None, 'tp'), P(), P(), P('tp', None))
    specs_out = (P(('dp', 'tp'), None), P(('dp', 'tp'), None), P('dp', 'tp'), P('dp', 'tp'), P('dp', 'tp'), P(('dp', 'tp'), None), P('dp'))
    return jax.shard_map(device_step, mesh=mesh, in_specs=specs_in, out_specs=specs_out, check_vma=False)
```

time: 468 us -> 316 us (0.68)
  Pallas kernels: 0 us -> 297 us
  matrix products: 185 us -> 0 us
  waiting for transfers between devices: 168 us -> 0 us
  blocking collectives: 44.4 us -> 0 us
  other arithmetic: 33.1 us -> 1.88 us
  between operations: 14.4 us -> 0.69 us
    pallas_call x0 -> x3, Pallas kernels: none -> 297 us  [the longest x1 140 us: device_step(): pl.pallas_call(functools.partial(fwd_kernel, tp, kvr), out_shape=[full, f...]
    dot_general x36 -> x0, matrix products: 173 us -> none  [the longest x12 31.3 us: one_block(): jnp.einsum('hqs,sd->qhd', prob_blk, v_raw, preferred_element_type=jnp.flo...]
    all_gather x2 -> x0, waiting for transfers between devices: 136 us -> none  [the longest x1 76.4 us: device_step(): h_full = lax.all_gather(hidden, 'tp', axis=0, tiled=True)]
    psum x1 -> x0, blocking collectives: 44.4 us -> none  [device_step(): d_gain = lax.psum(dg_part, 'tp')]
    reduce_scatter x2 -> x0, waiting for transfers between devices: 31.4 us -> none  [the longest x1 31.4 us: device_step(): mix_rows = lax.psum_scatter(mix_part, 'tp', scatter_dimension=0, tiled=True)]
    sub x4 -> x0, matrix products: 11.5 us -> none  [one_block(): prob_blk = jax.nn.softmax(scores, axis=-1).astype(jnp.bfloat16)]
    unnamed x30 -> x19, local copies, waits for them, and re-layouts: 5.12 us -> 15.7 us
    reduce_sum x6 -> x0, other arithmetic: 6.83 us -> none  [the longest x4 3.71 us: one_block(): prob_blk = jax.nn.softmax(scores, axis=-1).astype(jnp.bfloat16)]
  transfers between devices with their start and end apart: 6 -> 0, of which waited for: 3 -> 0; matrix products, arithmetic and copies ran while one was open for 19% -> 0% of each run, Pallas kernels for 0% -> 0%
where the time goes in v1:
time: 316 us; the launch traced here: 315 us
  Pallas kernels  297 us (94%)
  local copies, waits for them, and re-layouts  15.7 us (5%)
    pallas_call x1, Pallas kernels, device_step(): pl.pallas_call(functools.partial(fwd_kernel, tp, kvr), out_shape=[full, f...  140 us
    pallas_call x1, Pallas kernels, device_step(): pl.pallas_call(functools.partial(grad_kernel, tp), out_shape=[sds((rows,...  83.4 us
    pallas_call x1, Pallas kernels, device_step(): pl.pallas_call(functools.partial(bwd_kernel, tp, kvr), out_shape=[sds((ro...  73.7 us
    unnamed x19, local copies, waits for them, and re-layouts  15.7 us

profile of v1, /device:TPU:21, one launch (start us, length us, event | category | flops | bytes accessed | tf_op | source)
XLA Modules:
  0.0 315.5 jit_solution(12719792274545371260)
XLA Ops:
  0.6 1.3 convert_bitcast_fusion.pos_ref
  1.9 0.6 maximum_bitcast_fusion.frq_ref
  2.5 140.2 %gather_fwd.1 = (bf16[1024,6144]{1,0:T(8,128)(2,1)}, bf16[1024,6144]{1,0:T(8,128)(2,1)}, bf16[8,64,6144]{2,1,0:T(8,128)(2,1)}, bf16[8,64,6144]{2,1,0:T(8,128)(2,...) custom-call(bf16[64,6144]{1,0:T(8,128)(2,1)} %x_ref.5, ...), custom_call_target="tpu_custom_call" | custom-call | tf_op jit(solution)/shard_map/gather_fwd/pallas_call | solution.py:674
  142.7 73.7 %scatter_bwd.1 = (bf16[64,6144]{1,0:T(8,128)(2,1)}, bf16[1024,640]{1,0:T(8,128)(2,1)}, bf16[8,64,6144]{2,1,0:T(8,128)(2,1)}, bf16[8,64,6144]{2,1,0:T(8,128)(2,1)}) custom-call(bf16[8,64,6144]{2,1,0:T(8,128)(2,1)} %get-tuple-element.30.mix_own, bf16[8,64,6144]{2,1,0:T(8,128)(2,1)} %get-tuple-element.31.mix_peer, bf16[64,6144]{1,0:T(8,128)(2,1)} %x_ref.5, ...), custom_call_target="tpu_custom_call" | custom-call | tf_op jit(solution)/shard_map/scatter_bwd/pallas_call | solution.py:688
  216.4 0.0 copy-start.2
  216.4 83.4 %scatter_grads.1 = (bf16[64,6144]{1,0:T(8,128)(2,1)}, f32[1,6144]{1,0:T(1,128)}, bf16[6144,384]{1,0:T(8,128)(2,1)}, f32[6144,128]{1,0:T(8,128)}, f32[6144,128]{1,0:T(8,128)}, /*index=5*/bf16[384,6144]{1,0:T(8,128)(2,1)}) custom-call(bf16[8,64,6144]{2,1,0:T(8,128)(2,1)} %get-tuple-element.42.dh_own, bf16[8,64,6144]{2,1,0:T(8,128)(2,1)} %get-tuple-element.43.dh_peer, ...), custom_call_target="tpu_custom_call" | custom-call | tf_op jit(solution)/shard_map/scatter_grads/pallas_call | solution.py:702
  299.8 0.0 copy-done.2
  299.8 0.9 copy.22
  300.7 2.1 copy.23
  302.7 0.0 copy-start.1
  302.7 0.0 slice-start
  302.7 5.2 %copy.24 = bf16[6144,384]{1,0:T(8,128)(2,1)} copy(bf16[6144,384]{1,0:T(8,128)(2,1)} %get-tuple-element.62) | data formatting | bytes 9437184
  308.0 0.0 copy-done.1
  308.0 0.0 copy-start
  308.0 0.0 slice-start.1
  308.0 1.7 copy.25
  309.6 1.4 copy-done
  311.0 1.7 copy.26
  312.7 0.0 slice-done
  312.7 0.0 slice-done.1
  312.7 0.0 copy-start.3
  312.7 2.2 copy.27
  314.9 0.0 copy-done.3
  314.9 0.6 copy.28
  (2 shorter events, 0.0 us)
Async XLA Ops:
  216.4 83.4 %copy-start.2 = (bf16[64,6144]{1,0:T(8,128)(2,1)S(1)}, bf16[64,6144]{1,0:T(8,128)(2,1)}, u32[]{:S(2)}) copy-start(bf16[64,6144]{1,0:T(8,128)(2,1)} %get-tuple-element.60) | copy-start | bytes 2359300
  302.7 5.2 %copy-start.1 = (f32[6144,128]{1,0:T(8,128)S(1)}, f32[6144,128]{1,0:T(8,128)}, u32[]{:S(2)}) copy-start(f32[6144,128]{1,0:T(8,128)} %get-tuple-element.63) | copy-start | bytes 9437188
  302.7 9.9 %slice-start = ((s8[4718592]{0:T(1024)(128)(4,1)}), s8[4194304]{0:T(1024)(128)(4,1)S(1)}, s32[]{:S(2)}) async-start(s8[4718592]{0:T(1024)(128)(4,1)} %bitcast.6), calls=%async_computation | async-start | bytes 8388608
  308.0 3.0 copy-start
  308.0 4.7 %slice-start.1 = ((s8[4718592]{0:T(1024)(128)(4,1)}), s8[524288]{0:T(1024)(128)(4,1)S(1)}, s32[]{:S(2)}) async-start(s8[4718592]{0:T(1024)(128)(4,1)} %bitcast.6), calls=%async_computation.1 | async-start | bytes 1048576
  312.7 2.2 copy-start.3

commit v2 on v1

v2 whole, which is shorter than its diff:
```python
import functools
import jax
import jax.numpy as jnp
import numpy as np
from jax import lax
from jax.experimental import pallas as pl
from jax.experimental.pallas import tpu as pltpu
from jax.sharding import PartitionSpec as P

HEAD_DIM = 128
TILE = 128
SUBS = 4
SCORE_SCALE = HEAD_DIM ** -0.5
ROPE_THETA = 1000000.0
NORM_EPS = 1e-05
MASKED = -1e30
MESH = pl.DeviceIdType.MESH
F32 = jnp.float32
BF16 = jnp.bfloat16
ANY = pl.BlockSpec(memory_space=pl.ANY)
VM = pl.BlockSpec(memory_space=pltpu.VMEM)
NT = (((1,), (1,)), ((), ()))
TN = (((0,), (0,)), ((), ()))
VMEM_LIMIT = 63 * 1024 * 1024


def dot(a, b, dims=(((1,), (0,)), ((), ()))):
    return lax.dot_general(a, b, dims, preferred_element_type=F32)


class Ring:
    def __init__(self, tp):
        self.tp = tp
        self.nz = tp // 2
        self.me = lax.axis_index("tp")
        self.c = self.me // 2
        self.k = self.me % 2
        self.up = lax.rem(self.c + 1, self.nz) * 2 + self.k
        self.dn = lax.rem(self.c + self.nz - 1, self.nz) * 2 + self.k
        self.pt = self.c * 2 + 1 - self.k

    def barrier(self):
        bar = pltpu.get_barrier_semaphore()
        for d in (self.up, self.dn, self.pt):
            pl.semaphore_signal(bar, inc=1, device_id={"tp": d}, device_id_type=MESH)
        pl.semaphore_wait(bar, 3)

    def barrier_all(self):
        bar = pltpu.get_barrier_semaphore()
        for o in range(1, self.tp):
            pl.semaphore_signal(bar, inc=1, device_id={"tp": lax.rem(self.me + o, self.tp)}, device_id_type=MESH)
        pl.semaphore_wait(bar, self.tp - 1)

    def chip(self, n):
        return lax.rem(n + 2 * self.nz, self.nz)


def remote(src, dst, ss, rs, dev):
    return pltpu.make_async_remote_copy(src, dst, ss, rs, device_id={"tp": dev}, device_id_type=MESH)


class Gather:
    def __init__(self, rg, src, dst, rows, ss, rs, dss, drs, ls):
        self.rg, self.src, self.dst, self.R = rg, src, dst, rows
        self.ss, self.rs, self.dss, self.drs, self.ls = ss, rs, dss, drs, ls
        self.H = rows // 2
        self.steps = rg.nz - 1

    def rows(self, chip, core, half):
        return pl.ds(pl.multiple_of((self.rg.chip(chip) * 2 + core) * self.R + half * self.H, self.H), self.H)

    def half(self, d, s):
        return s % 2 if d == 0 else 1 - s % 2

    def origin(self, d, s):
        h = (s + 2) // 2
        return self.rg.c - h if d == 0 else self.rg.c + h

    def dev(self, d):
        return self.rg.up if d == 0 else self.rg.dn

    def own(self, d, s):
        h = self.half(d, s)
        return remote(self.src.at[pl.ds(h * self.H, self.H), :], self.dst.at[self.rows(self.rg.c, self.rg.k, h), :],
                      self.ss.at[d, s], self.rs.at[d, s], self.dev(d))

    def recv_rows(self, d, s, core):
        return self.rows(self.origin(d, s), core, self.half(d, s))

    def fwd(self, d, s):
        r = self.recv_rows(d, s - 2, self.rg.k)
        return remote(self.dst.at[r, :], self.dst.at[r, :], self.ss.at[d, s], self.rs.at[d, s], self.dev(d))

    def recv(self, d, s):
        r = self.recv_rows(d, s, self.rg.k)
        return remote(self.dst.at[r, :], self.dst.at[r, :], self.ss.at[d, s], self.rs.at[d, s], self.dev(d))

    def pair(self, i, r):
        return remote(self.dst.at[r, :], self.dst.at[r, :], self.dss.at[i], self.drs.at[i], self.rg.pt)

    def block(self, dev):
        return pl.ds(pl.multiple_of(dev * self.R, self.R), self.R)

    def pair_own(self):
        return remote(self.src, self.dst.at[self.block(self.rg.me), :], self.dss.at[0], self.drs.at[0], self.rg.pt)

    def local(self):
        return pltpu.make_async_copy(self.src, self.dst.at[self.block(self.rg.me), :], self.ls)

    def start_ring(self, s):
        for d in range(2):
            self.own(d, s).start()

    def start_local(self):
        self.local().start()
        self.pair_own().start()

    def tick(self, s, forward=True):
        for d in range(2):
            self.recv(d, s).wait_recv()
            if isinstance(s, int):
                if s + 2 < self.steps:
                    self.fwd(d, s + 2).start()
            else:
                @pl.when(s + 2 < self.steps)
                def _():
                    self.fwd(d, s + 2).start()
            self.pair(1 + 2 * s + d, self.recv_rows(d, s, self.rg.k)).start()

    def wait_pair(self):
        self.local().wait()
        self.pair(0, self.block(self.rg.pt)).wait_recv()
        for s in range(self.steps):
            for d in range(2):
                self.pair(1 + 2 * s + d, self.recv_rows(d, s, 1 - self.rg.k)).wait_recv()

    def drain(self):
        self.pair_own().wait_send()
        for s in range(self.steps):
            for d in range(2):
                self.pair(1 + 2 * s + d, self.recv_rows(d, s, self.rg.k)).wait_send()
                if s < 2:
                    self.own(d, s).wait_send()
                else:
                    self.fwd(d, s).wait_send()

    @staticmethod
    def scratch(tp):
        n = tp // 2 - 1
        dma = pltpu.SemaphoreType.DMA
        return [dma((2, n)), dma((2, n)), dma((1 + 2 * n,)), dma((1 + 2 * n,)), dma]


class Scatter:
    def __init__(self, rg, own, peer, off, pre, psem, buf, ss, rs, final):
        self.rg, self.own, self.peer, self.pre, self.psem = rg, own, peer, pre, psem
        self.buf, self.ss, self.rs, self.final = buf, ss, rs, final
        self.H = own.shape[-1] // 2
        self.W = pre.shape[-1]
        self.off = off
        self.CW = self.W // SUBS

    def blk(self, d, s):
        return self.rg.chip(self.rg.c - 1 - s) if d == 0 else self.rg.chip(self.rg.c + 1 + s)

    def load(self, w, d, s):
        src = (self.own, self.peer)[w].at[self.blk(d, s), :, pl.ds(d * self.H + self.off, self.W)]
        return pltpu.make_async_copy(src, self.pre.at[s % 2, w, d], self.psem.at[s % 2, w, d])

    def start_loads(self, s):
        for w in range(2):
            for d in range(2):
                self.load(w, d, s).start()

    def wait_loads(self, s):
        for w in range(2):
            for d in range(2):
                self.load(w, d, s).wait()

    def send(self, d, u, s):
        return remote(self.buf.at[d, u, s], self.buf.at[d, u, s + 1], self.ss.at[d, u, s], self.rs.at[d, u, s],
                      self.rg.up if d == 0 else self.rg.dn)

    def cols(self, u):
        return pl.ds(u * self.CW if isinstance(u, int) else pl.multiple_of(u * self.CW, self.CW), self.CW)

    def mine(self, d, s, u):
        c = self.cols(u)
        return self.pre[s % 2, 0, d, :, c].astype(F32) + self.pre[s % 2, 1, d, :, c].astype(F32)

    def init(self):
        self.wait_loads(0)
        self.start_loads(1)
        for u in range(SUBS):
            for d in range(2):
                self.buf[d, u, 0] = self.mine(d, 0, u).astype(BF16)
                self.send(d, u, 0).start()

    def tick(self, s, u):
        last = self.rg.nz - 1

        def loads():
            self.wait_loads(s)

            @pl.when(s < last)
            def _():
                self.start_loads(s + 1)

        if isinstance(u, int):
            if u == 0:
                loads()
        else:
            pl.when(u == 0)(loads)
        for d in range(2):
            self.send(d, u, s - 1).wait_recv()

            @pl.when(s < last)
            def _():
                self.buf[d, u, s] = (self.mine(d, s, u) + self.buf[d, u, s].astype(F32)).astype(BF16)
                self.send(d, u, s).start()

            @pl.when(s == last)
            def _():
                self.final(d, u, self.mine(d, s, u) + self.buf[d, u, s].astype(F32))

    def drain(self):
        @pl.loop(0, self.rg.nz - 1)
        def _(s):
            for d in range(2):
                for u in range(SUBS):
                    self.send(d, u, s).wait_send()

    @staticmethod
    def scratch(tp, rows, W):
        nz = tp // 2
        dma = pltpu.SemaphoreType.DMA
        return [pltpu.VMEM((2, 2, 2, rows, W), BF16), dma((2, 2, 2)), pltpu.VMEM((2, SUBS, nz, rows, W // SUBS), BF16),
                dma((2, SUBS, nz - 1)), dma((2, SUBS, nz - 1))]


def weight_copies(kv, wq, wk, wv, wo, w_all, wo_v, sem):
    dq = wq.shape[1]
    kvc = pl.ds(pl.multiple_of(kv * HEAD_DIM, HEAD_DIM), HEAD_DIM)
    return [pltpu.make_async_copy(wq, w_all.at[:, pl.ds(0, dq)], sem.at[0]),
            pltpu.make_async_copy(wk.at[:, kvc], w_all.at[:, pl.ds(dq, HEAD_DIM)], sem.at[1]),
            pltpu.make_async_copy(wv.at[:, kvc], w_all.at[:, pl.ds(dq + HEAD_DIM, HEAD_DIM)], sem.at[2]),
            pltpu.make_async_copy(wo, wo_v, sem.at[3])]


def rope(t, cos, sin):
    return t * cos + pltpu.roll(t, HEAD_DIM // 2, 1) * sin


def rope_t(t, cos, sin):
    return t * cos - pltpu.roll(t, HEAD_DIM // 2, 1) * sin


def to_col(row):
    return jnp.broadcast_to(row, (TILE, TILE)).T


def trow(i, n=TILE):
    return pl.ds(pl.multiple_of(i * n, n), n)


def keep_t(kdc, kdr, i, seq):
    key = lax.broadcasted_iota(jnp.int32, (seq, TILE), 0)
    qry = lax.broadcasted_iota(jnp.int32, (seq, TILE), 1) + i * TILE
    return (key <= qry) & (kdc == kdr)


def first_kernel(tp, kvr, x_ref, g_ref, pos_ref, frq_ref, dy_ref, wq, wk, wv, wo,
                 h_full, dy_full, mix_own, mix_peer, dh_own, dh_peer, ot_ref, dqkv_ref, out_ref,
                 hown, w_all, wo_v, tile, stage, q3_ref, k_ref, v_ref, vt, kt, st_ref, cos_ref, sin_ref, kdc_ref, kdr_ref,
                 dk_acc, dv_acc, do3, dqkv_t, wsem, tsem, msem, mss, mrs, dsem, dss, drs, *sems):
    rg = Ring(tp)
    rows, dm = x_ref.shape
    seq = rows * tp
    nt = seq // TILE
    np_ = nt // 2
    dq = wq.shape[1]
    nh = dq // HEAD_DIM
    half = TILE // 2
    ga = Gather(rg, hown, h_full, rows, *sems[:5])
    gd = Gather(rg, dy_ref, dy_full, rows, *sems[5:10])

    def final(d, u, val):
        xs = pl.ds(pl.multiple_of(d * sc.H + u * sc.CW, sc.CW), sc.CW)
        out_ref[d, :, sc.cols(u)] = (x_ref[:, xs].astype(F32) + val).astype(BF16)

    sc = Scatter(rg, mix_own, mix_peer, 0, *sems[10:], final)
    wcp = weight_copies(rg.me // kvr, wq, wk, wv, wo, w_all, wo_v, wsem)
    for cp in wcp:
        cp.start()
    RB = 16

    @pl.loop(0, rows // RB)
    def _(r):
        xf = x_ref[trow(r, RB), :].astype(F32)
        inv = lax.rsqrt(jnp.mean(xf * xf, axis=-1, keepdims=True) + NORM_EPS)
        hown[trow(r, RB), :] = (xf * inv * g_ref[...]).astype(BF16)

    rg.barrier()
    ga.start_ring(0)
    ga.start_ring(1)
    ga.start_local()
    gd.start_local()
    lane = lax.broadcasted_iota(jnp.int32, (TILE, TILE), 1)
    sgn = jnp.where(lane < HEAD_DIM // 2, -1.0, 1.0).astype(F32)
    kdr_ref[...] = (pos_ref[...] - (lax.broadcasted_iota(jnp.int32, pos_ref.shape, 0) * TILE
                                    + lax.broadcasted_iota(jnp.int32, pos_ref.shape, 1))).astype(F32)

    @pl.loop(0, nt)
    def _(i):
        ang = to_col(pos_ref[pl.ds(i, 1), :].astype(F32)) * frq_ref[...]
        cos_ref[trow(i), :] = jnp.cos(ang)
        sin_ref[trow(i), :] = jnp.sin(ang) * sgn
        kdc_ref[trow(i), :] = to_col(kdr_ref[pl.ds(i, 1), :])

    dk_acc[...] = jnp.zeros_like(dk_acc)
    dv_acc[...] = jnp.zeros_like(dv_acc)
    for s in range(ga.steps):
        ga.tick(s)
        if s >= ga.steps - 2:
            gd.start_ring(s - (ga.steps - 2))
    ga.wait_pair()
    for cp in wcp:
        cp.wait()

    def hload(i):
        return pltpu.make_async_copy(h_full.at[trow(i, 2 * TILE), :], tile.at[i % 2], tsem.at[i % 2])

    hload(0).start()

    @pl.loop(0, np_)
    def _(p):
        hload(p).wait()

        @pl.when(p + 1 < np_)
        def _():
            hload(p + 1).start()

        @pl.when(p == np_ // 2)
        def _():
            gd.tick(0)
        qkv = dot(tile[p % 2], w_all[...])
        for j in range(2):
            i = 2 * p + j
            js = slice(j * TILE, (j + 1) * TILE)
            cos, sin = cos_ref[trow(i), :], sin_ref[trow(i), :]
            for h in range(nh + 1):
                t = qkv[js, h * HEAD_DIM:(h + 1) * HEAD_DIM].astype(BF16).astype(F32)
                t = rope(t, cos, sin)
                if h < nh:
                    q3_ref[i, pl.ds(h * TILE, TILE), :] = t.astype(BF16)
                else:
                    k_ref[trow(i), :] = t.astype(BF16)
                    kt[:, trow(i)] = t.T.astype(BF16)
            v = qkv[js, (nh + 1) * HEAD_DIM:]
            v_ref[trow(i), :] = v.astype(BF16)
            vt[:, trow(i)] = v.T.astype(BF16)

    def half_rows(j, core):
        return pl.ds(pl.multiple_of(j * TILE + core * half, half), half)

    def mix_mine(i):
        return pltpu.make_async_copy(stage.at[i % 2, half_rows(0, rg.k), :], mix_own.at[i], msem.at[i % 2])

    def mix_other(i):
        return remote(stage.at[i % 2, half_rows(0, 1 - rg.k), :], mix_peer.at[i], mss.at[i], mrs.at[i], rg.pt)

    NC = dm // 4

    @pl.loop(0, nt)
    def _(i):
        for n in range(2):
            @pl.when(i == n * np_)
            def _():
                gd.tick(1 + n)

        s = dot(k_ref[...], q3_ref[i], NT) * SCORE_SCALE
        keep = keep_t(kdc_ref[...], kdr_ref[pl.ds(i, 1), :], i, seq)
        pbs = []
        for h in range(nh):
            sh = jnp.where(keep, s[:, h * TILE:(h + 1) * TILE], MASKED)
            m = jnp.max(sh, axis=0, keepdims=True)
            e = jnp.exp(sh - m)
            li = 1.0 / jnp.sum(e, axis=0, keepdims=True)
            st_ref[i, pl.ds(0, 1), pl.ds(h * TILE, TILE)] = m
            st_ref[i, pl.ds(1, 1), pl.ds(h * TILE, TILE)] = li
            pbs.append((e * li).astype(BF16))
        ot = dot(vt[...], jnp.concatenate(pbs, axis=1))
        os = []
        for h in range(nh):
            oh = ot[:, h * TILE:(h + 1) * TILE]
            ot_ref[pl.ds(h * HEAD_DIM, HEAD_DIM), trow(i)] = oh.astype(BF16)
            os.append(oh.T.astype(BF16))
        o = jnp.concatenate(os, axis=1)

        @pl.when(i >= 2)
        def _():
            mix_mine(i - 2).wait()
            mix_other(i - 2).wait_send()
        for n in range(4):
            ns = pl.ds(n * NC, NC)
            stage[i % 2, pl.ds(0, TILE), ns] = dot(o, wo_v[:, ns]).astype(BF16)
        mix_mine(i).start()
        mix_other(i).start()

    for i in (nt - 2, nt - 1):
        mix_mine(i).wait()
        mix_other(i).wait_send()
    for i in range(nt):
        mix_other(i).wait_recv()
    sc.start_loads(0)
    for s in range(3, gd.steps - 2):
        gd.tick(s)
    sc.init()
    for s in range(max(3, gd.steps - 2), gd.steps):
        gd.tick(s)
    gd.wait_pair()

    def yload(it):
        return pltpu.make_async_copy(dy_full.at[trow(np_ - 1 - it, 2 * TILE), :], tile.at[it % 2], tsem.at[it % 2])

    def dh_mine(i, sl, j):
        return pltpu.make_async_copy(stage.at[sl, half_rows(j, rg.k), :], dh_own.at[i], dsem.at[sl, j])

    def dh_other(i, sl, j):
        return remote(stage.at[sl, half_rows(j, 1 - rg.k), :], dh_peer.at[i], dss.at[i], drs.at[i], rg.pt)

    def attn(i, j):
        q3 = q3_ref[i]
        do = do3[j]
        s = dot(k_ref[...], q3, NT) * SCORE_SCALE
        keep = keep_t(kdc_ref[...], kdr_ref[pl.ds(i, 1), :], i, seq)
        dp = dot(v_ref[...], do, NT)
        pbs, dss_ = [], []
        for h in range(nh):
            hs = slice(h * TILE, (h + 1) * TILE)
            m = st_ref[i, pl.ds(0, 1), pl.ds(h * TILE, TILE)]
            li = st_ref[i, pl.ds(1, 1), pl.ds(h * TILE, TILE)]
            p = jnp.exp(jnp.where(keep, s[:, hs], MASKED) - m) * li
            dph = dp[:, hs].astype(BF16).astype(F32)
            dl = jnp.sum(dph * p, axis=0, keepdims=True)
            dss_.append((p * (dph - dl) * SCORE_SCALE).astype(BF16))
            pbs.append(p.astype(BF16))
        pb = jnp.concatenate(pbs, axis=1)
        ds = jnp.concatenate(dss_, axis=1)
        dv_acc[...] += dot(pb, do)
        dk_acc[...] += dot(ds, q3)
        dqt = dot(kt[...], ds)
        cos, sin = cos_ref[trow(i), :], sin_ref[trow(i), :]
        jr = pl.ds(j * TILE, TILE)
        for h in range(nh):
            t = dqt[:, h * TILE:(h + 1) * TILE].T.astype(BF16).astype(F32)
            dqkv_t[jr, pl.ds(h * HEAD_DIM, HEAD_DIM)] = rope_t(t, cos, sin).astype(BF16)
        t = dk_acc[trow(i), :].astype(BF16).astype(F32)
        dqkv_t[jr, pl.ds(dq, HEAD_DIM)] = rope_t(t, cos, sin).astype(BF16)
        dqkv_t[jr, pl.ds(dq + HEAD_DIM, HEAD_DIM)] = dv_acc[trow(i), :].astype(BF16)

    yload(0).start()
    per = -(-SUBS * (rg.nz - 1) // np_)

    @pl.loop(0, np_)
    def _(it):
        ip = np_ - 1 - it
        sl = it % 2
        yload(it).wait()

        @pl.when(it + 1 < np_)
        def _():
            yload(it + 1).start()

        def tick(n):
            at = per * it + n
            sc.tick(1 + at // SUBS, at % SUBS)

        do = dot(tile[sl], wo_v[...], NT).astype(BF16)
        for j in range(2):
            for h in range(nh):
                do3[j, pl.ds(h * TILE, TILE), :] = do[j * TILE:(j + 1) * TILE, h * HEAD_DIM:(h + 1) * HEAD_DIM]
        tick(0)
        attn(2 * ip + 1, 1)
        tick(1)
        attn(2 * ip, 0)
        tick(2)
        dqkv_ref[trow(ip, 2 * TILE), :] = dqkv_t[...]

        @pl.when(it >= 2)
        def _():
            for j in range(2):
                dh_mine(2 * (ip + 2) + j, sl, j).wait()
                dh_other(2 * (ip + 2) + j, sl, j).wait_send()
        for n in range(4):
            ns = pl.ds(n * NC, NC)
            stage[sl, :, ns] = dot(dqkv_t[...], w_all[ns, :], NT).astype(BF16)
            if n == 3:
                for j in range(2):
                    dh_mine(2 * ip + j, sl, j).start()
                    dh_other(2 * ip + j, sl, j).start()
            tick(3 + n)

    for it in (np_ - 2, np_ - 1):
        ip = np_ - 1 - it
        for j in range(2):
            dh_mine(2 * ip + j, it % 2, j).wait()
            dh_other(2 * ip + j, it % 2, j).wait_send()
    for i in range(nt):
        dh_other(i, 0, 0).wait_recv()
    sc.drain()
    ga.drain()
    gd.drain()


def second_kernel(tp, dh_own, dh_peer, mix_own, mix_peer, part1_ref, x_ref, dy_ref, g_ref, h_full, dy_full, dqkv_ref, ot_ref,
                  out_ref, gx_ref, dg_ref, dwq, dwk, dwv, dwo,
                  ht, yt, skv, peer, dhr, part, slots, tot, hsem, ysem, pss, prs, gss, grs, bss, brs, *rsem):
    rg = Ring(tp)
    rows, dm = x_ref.shape
    nz = rg.nz
    dq = dwq.shape[1]
    CB = dm // nz
    LAG = 5
    done = part1_ref.shape[-1]

    def final_a(d, u, val):
        dhr[:, pl.ds(d * sa.H + u * sa.CW, sa.CW)] = val.astype(BF16)

    def final_b(d, u, val):
        cs = pl.ds(d * sb.H + sb.off + u * sb.CW, sb.CW)
        out_ref[:, cs] = (x_ref[:, cs].astype(F32) + val).astype(BF16)

    sa = Scatter(rg, dh_own, dh_peer, 0, *rsem[:5], final_a)
    sb = Scatter(rg, mix_own, mix_peer, done, *rsem[5:], final_b)
    sa.start_loads(0)
    sb.start_loads(0)

    def col(it, n=None):
        return pl.ds(pl.multiple_of(it * CB, CB), CB)

    def hload(it):
        return pltpu.make_async_copy(h_full.at[:, col(it)], ht.at[it % 2], hsem.at[it % 2])

    def yload(it):
        return pltpu.make_async_copy(dy_full.at[:, col(it)], yt.at[it % 2], ysem.at[it % 2])

    hload(0).start()
    yload(0).start()
    rg.barrier_all()
    sa.init()
    for d in range(2):
        out_ref[:, pl.ds(d * sb.H, done)] = part1_ref[d]

    def to_peer(it):
        return remote(skv.at[it % 2], peer.at[it], pss.at[it], prs.at[it], rg.pt)

    def pair_sum(it):
        to_peer(it).wait_recv()
        both = peer[it] + skv[it % 2]
        dwk[col(it), :] = both[:, :HEAD_DIM]
        dwv[col(it), :] = both[:, HEAD_DIM:]
        to_peer(it).wait_send()

    HC = CB // 2

    @pl.loop(0, nz)
    def _(it):
        sl = it % 2
        hload(it).wait()
        yload(it).wait()

        @pl.when(it + 1 < nz)
        def _():
            hload(it + 1).start()
            yload(it + 1).start()

        @pl.when(it == LAG)
        def _():
            sb.init()

        def tick(u):
            @pl.when(it > 0)
            def _():
                sa.tick(it, u)

            @pl.when(it > LAG)
            def _():
                sb.tick(it - LAG, u)

        for n in range(2):
            tick(2 * n)
            hs = pl.ds(n * HC, HC)
            at = pl.ds(pl.multiple_of(it * CB + n * HC, HC), HC)
            dw = dot(ht[sl, :, hs], dqkv_ref[...], TN)
            dwq[at, :] = dw[:, :dq].astype(BF16)
            skv[sl, hs, :] = dw[:, dq:]
            tick(2 * n + 1)
            dwo[:, at] = dot(ot_ref[...], yt[sl, :, hs]).astype(BF16)
        to_peer(it).start()

        @pl.when(it >= 1)
        def _():
            pair_sum(it - 1)

    for u in range(SUBS):
        sb.tick(nz - LAG, u)
    RB = 16
    part[...] = jnp.zeros_like(part)

    @pl.loop(0, rows // RB)
    def _(r):
        rr = trow(r, RB)
        xf = x_ref[rr, :].astype(F32)
        inv = lax.rsqrt(jnp.mean(xf * xf, axis=-1, keepdims=True) + NORM_EPS)
        xh = xf * inv
        dh = dhr[rr, :].astype(F32)
        part[...] += jnp.sum(dh * xh, axis=0, keepdims=True)
        a = dh * g_ref[...]
        di = inv * (a - xh * jnp.mean(a * xh, axis=-1, keepdims=True))
        gx_ref[rr, :] = (dy_ref[rr, :].astype(F32) + di).astype(BF16)

    GW = dm // tp

    def gcol(dev):
        return pl.ds(pl.multiple_of(dev * GW, GW), GW)

    def dev(o):
        return lax.rem(rg.me + o, tp)

    def scat(o):
        return remote(part.at[:, gcol(dev(o))], slots.at[o], gss.at[o], grs.at[o], dev(o))

    for o in range(1, tp):
        scat(o).start()
    pair_sum(nz - 1)
    rest = list(range(nz - LAG + 1, nz))
    for s in rest[:2]:
        for u in range(SUBS):
            sb.tick(s, u)
    acc = part[:, gcol(rg.me)]
    for o in range(1, tp):
        scat(o).wait_recv()
        acc = acc + slots[o]
    tot[...] = acc

    def bcast(o):
        return remote(tot, dg_ref.at[:, gcol(rg.me)], bss.at[o], brs.at[o], dev(o))

    def arrive(o):
        src = lax.rem(rg.me + tp - o, tp)
        return remote(tot, dg_ref.at[:, gcol(src)], bss.at[o], brs.at[o], dev(o))

    for o in range(1, tp):
        bcast(o).start()
    dg_ref[:, gcol(rg.me)] = acc
    for s in rest[2:]:
        for u in range(SUBS):
            sb.tick(s, u)
    for o in range(1, tp):
        arrive(o).wait_recv()
    for o in range(1, tp):
        scat(o).wait_send()
        bcast(o).wait_send()
    sa.drain()
    sb.drain()


def solution(mesh):
    tp = mesh.shape["tp"]
    nz = tp // 2
    DMA = pltpu.SemaphoreType.DMA

    def device_step(x, dy, pos, gain, wq, wk, wv, wo):
        rows, dm = x.shape
        seq = rows * tp
        nt = seq // TILE
        dq = wq.shape[1]
        nh = dq // HEAD_DIM
        qr = nh * TILE
        wd = dq + 2 * HEAD_DIM
        kvr = tp // (wk.shape[1] // HEAD_DIM)
        expo = np.arange(0, HEAD_DIM, 2, dtype=np.float64) / HEAD_DIM
        frq = (ROPE_THETA ** -expo).astype(np.float32)
        frq = jnp.asarray(np.concatenate([frq, frq]).reshape(1, HEAD_DIM))
        g2 = gain.reshape(1, dm)
        pos2 = pos.reshape(nt, TILE)

        def sds(shape, dt):
            return jax.ShapeDtypeStruct(shape, dt)

        V = pltpu.VMEM
        full = sds((seq, dm), BF16)
        blocks = sds((nt, rows, dm), BF16)
        W1 = dm // 3
        W2 = dm // 2 - W1
        h_full, dy_full, mix_own, mix_peer, dh_own, dh_peer, ot, dqkv, part1 = pl.pallas_call(
            functools.partial(first_kernel, tp, kvr),
            out_shape=[full, full, blocks, blocks, blocks, blocks, sds((dq, seq), BF16), sds((seq, wd), BF16), sds((2, rows, W1), BF16)],
            in_specs=[VM, VM, VM, VM, ANY, ANY, ANY, ANY, ANY],
            out_specs=[ANY] * 6 + [VM] * 3,
            scratch_shapes=[V((rows, dm), BF16), V((dm, wd), BF16), V((dq, dm), BF16), V((2, 2 * TILE, dm), BF16), V((2, 2 * TILE, dm), BF16),
                            V((nt, qr, HEAD_DIM), BF16), V((seq, HEAD_DIM), BF16), V((seq, HEAD_DIM), BF16), V((HEAD_DIM, seq), BF16),
                            V((HEAD_DIM, seq), BF16), V((nt, 2, qr), F32), V((seq, HEAD_DIM), F32), V((seq, HEAD_DIM), F32), V((seq, TILE), F32),
                            V((nt, TILE), F32), V((seq, HEAD_DIM), F32), V((seq, HEAD_DIM), F32), V((2, qr, HEAD_DIM), BF16),
                            V((2 * TILE, wd), BF16), DMA((4,)), DMA((2,)), DMA((2,)), DMA((nt,)), DMA((nt,)), DMA((2, 2)), DMA((nt,)), DMA((nt,))]
            + Gather.scratch(tp) + Gather.scratch(tp) + Scatter.scratch(tp, rows, W1),
            compiler_params=pltpu.CompilerParams(collective_id=1, has_side_effects=True, vmem_limit_bytes=VMEM_LIMIT),
            name="gather_attend_scatter",
        )(x, g2, pos2, frq, dy, wq, wk, wv, wo)

        CB = dm // nz
        out, grad_x, d_gain, d_wq, d_wk, d_wv, d_wo = pl.pallas_call(
            functools.partial(second_kernel, tp),
            out_shape=[sds((rows, dm), BF16), sds((rows, dm), BF16), sds((1, dm), F32), V((dm, dq), BF16), V((dm, HEAD_DIM), F32),
                       V((dm, HEAD_DIM), F32), V((dq, dm), BF16)],
            in_specs=[ANY, ANY, ANY, ANY, VM, VM, VM, VM, ANY, ANY, VM, VM],
            out_specs=[VM] * 7,
            scratch_shapes=[V((2, seq, CB), BF16), V((2, seq, CB), BF16), V((2, CB, 2 * HEAD_DIM), F32), V((nz, CB, 2 * HEAD_DIM), F32),
                            V((rows, dm), BF16), V((1, dm), F32), V((tp, 1, dm // tp), F32), V((1, dm // tp), F32),
                            DMA((2,)), DMA((2,)), DMA((nz,)), DMA((nz,)), DMA((tp,)), DMA((tp,)), DMA((tp,)), DMA((tp,))]
            + Scatter.scratch(tp, rows, dm // 2) + Scatter.scratch(tp, rows, W2),
            compiler_params=pltpu.CompilerParams(collective_id=2, has_side_effects=True, vmem_limit_bytes=40 * 1024 * 1024),
            name="scatter_grads",
        )(dh_own, dh_peer, mix_own, mix_peer, part1, x, dy, g2, h_full, dy_full, dqkv, ot)
        return out, grad_x, d_wq, d_wk, d_wv, d_wo, d_gain.reshape(dm)

    specs_in = (P(('dp', 'tp'), None), P(('dp', 'tp'), None), P('dp'), P(), P(None, 'tp'), P(), P(), P('tp', None))
    specs_out = (P(('dp', 'tp'), None), P(('dp', 'tp'), None), P('dp', 'tp'), P('dp', 'tp'), P('dp', 'tp'), P(('dp', 'tp'), None), P('dp'))
    return jax.shard_map(device_step, mesh=mesh, in_specs=specs_in, out_specs=specs_out, check_vma=False)
```

time: 316 us -> 286 us (0.905)
  Pallas kernels: 297 us -> 274 us
  local copies, waits for them, and re-layouts: 15.7 us -> 10.1 us
    pallas_call x3 -> x2, Pallas kernels: 297 us -> 274 us  [the longest x1 181 us: device_step(): pl.pallas_call(functools.partial(first_kernel, tp, kvr), out_shape=[full,...]
    unnamed x19 -> x13, local copies, waits for them, and re-layouts: 15.7 us -> 10.1 us
where the time goes in v2:
time: 286 us; the launch traced here: 285 us
  Pallas kernels  274 us (96%)
  local copies, waits for them, and re-layouts  10.1 us (4%)
    pallas_call x1, Pallas kernels, device_step(): pl.pallas_call(functools.partial(first_kernel, tp, kvr), out_shape=[full,...  181 us
    pallas_call x1, Pallas kernels, device_step(): pl.pallas_call(functools.partial(second_kernel, tp), out_shape=[sds((rows...  93.8 us
    unnamed x13, local copies, waits for them, and re-layouts  10.1 us

profile of v2, /device:TPU:21, one launch (start us, length us, event | category | flops | bytes accessed | tf_op | source)
XLA Modules:
  0.0 285.1 jit_solution(3337875445169898682)
XLA Ops:
  0.6 180.5 %gather_attend_scatter.1 = (bf16[1024,6144]{1,0:T(8,128)(2,1)}, bf16[1024,6144]{1,0:T(8,128)(2,1)}, bf16[8,64,6144]{2,1,0:T(8,128)(2,1)}, bf16[8,64,6144]{2,1,0:...) custom-call(bf16[64,6144]{1,0:T(8,128)(2,1)} %x_ref.3, ...), custom_call_target="tpu_custom_call" | custom-call | tf_op jit(solution)/shard_map/gather_attend_scatter/pallas_call | solution.py:697
  181.2 93.8 %scatter_grads.1 = (bf16[64,6144]{1,0:T(8,128)(2,1)}, bf16[64,6144]{1,0:T(8,128)(2,1)}, f32[1,6144]{1,0:T(1,128)}, bf16[6144,384]{1,0:T(8,128)(2,1)S(1)}, f32[61...) custom-call(bf16[8,64,6144]{2,1,0:T(8,128)(2,1)} %get-tuple-element.23.dh_own, ...), custom_call_target="tpu_custom_call" | custom-call | tf_op jit(solution)/shard_map/scatter_grads/pallas_call | solution.py:713
  275.0 1.7 copy.24
  276.6 1.7 copy.25
  278.3 2.2 copy.23
  280.5 0.0 copy-start.1
  280.5 0.0 copy-start
  280.5 0.0 copy-start.2
  280.5 2.2 copy.26
  282.7 0.0 copy-done.1
  282.7 0.9 copy.27
  283.6 0.0 copy-done
  283.6 0.9 copy.28
  284.4 0.0 copy-done.2
  284.4 0.6 copy.29
Async XLA Ops:
  280.5 2.2 copy-start.1
  280.5 3.1 %copy-start = (bf16[64,6144]{1,0:T(8,128)(2,1)S(1)}, bf16[64,6144]{1,0:T(8,128)(2,1)}, u32[]{:S(2)}) copy-start(bf16[64,6144]{1,0:T(8,128)(2,1)} %get-tuple-element.54) | copy-start | bytes 2359300
  280.5 4.0 %copy-start.2 = (f32[1,6144]{1,0:T(1,128)S(1)}, f32[1,6144]{1,0:T(1,128)}, u32[]{:S(2)}) copy-start(f32[1,6144]{1,0:T(1,128)} %get-tuple-element.38) | copy-start | bytes 73732

commit v3 on v2

--- a/solution.py
+++ b/solution.py
@@ -39,17 +39,19 @@
         self.dn = lax.rem(self.c + self.nz - 1, self.nz) * 2 + self.k
         self.pt = self.c * 2 + 1 - self.k
 
-    def barrier(self):
+    def greet(self, devs):
         bar = pltpu.get_barrier_semaphore()
-        for d in (self.up, self.dn, self.pt):
+        for d in devs:
             pl.semaphore_signal(bar, inc=1, device_id={"tp": d}, device_id_type=MESH)
-        pl.semaphore_wait(bar, 3)
-
-    def barrier_all(self):
-        bar = pltpu.get_barrier_semaphore()
-        for o in range(1, self.tp):
-            pl.semaphore_signal(bar, inc=1, device_id={"tp": lax.rem(self.me + o, self.tp)}, device_id_type=MESH)
-        pl.semaphore_wait(bar, self.tp - 1)
+
+    def greet_near(self):
+        self.greet((self.up, self.dn, self.pt))
+
+    def greet_all(self):
+        self.greet([lax.rem(self.me + o, self.tp) for o in range(1, self.tp)])
+
+    def met(self, count):
+        pl.semaphore_wait(pltpu.get_barrier_semaphore(), count)
 
     def chip(self, n):
         return lax.rem(n + 2 * self.nz, self.nz)
@@ -223,8 +225,8 @@
             def _():
                 self.final(d, u, self.mine(d, s, u) + self.buf[d, u, s].astype(F32))
 
-    def drain(self):
-        @pl.loop(0, self.rg.nz - 1)
+    def drain(self, lo, hi):
+        @pl.loop(lo, hi)
         def _(s):
             for d in range(2):
                 for u in range(SUBS):
@@ -289,6 +291,7 @@
         out_ref[d, :, sc.cols(u)] = (x_ref[:, xs].astype(F32) + val).astype(BF16)
 
     sc = Scatter(rg, mix_own, mix_peer, 0, *sems[10:], final)
+    rg.greet_near()
     wcp = weight_copies(rg.me // kvr, wq, wk, wv, wo, w_all, wo_v, wsem)
     for cp in wcp:
         cp.start()
@@ -300,7 +303,7 @@
         inv = lax.rsqrt(jnp.mean(xf * xf, axis=-1, keepdims=True) + NORM_EPS)
         hown[trow(r, RB), :] = (xf * inv * g_ref[...]).astype(BF16)
 
-    rg.barrier()
+    rg.met(3)
     ga.start_ring(0)
     ga.start_ring(1)
     ga.start_local()
@@ -416,6 +419,7 @@
     for s in range(3, gd.steps - 2):
         gd.tick(s)
     sc.init()
+    ga.drain()
     for s in range(max(3, gd.steps - 2), gd.steps):
         gd.tick(s)
     gd.wait_pair()
@@ -423,11 +427,13 @@
     def yload(it):
         return pltpu.make_async_copy(dy_full.at[trow(np_ - 1 - it, 2 * TILE), :], tile.at[it % 2], tsem.at[it % 2])
 
-    def dh_mine(i, sl, j):
-        return pltpu.make_async_copy(stage.at[sl, half_rows(j, rg.k), :], dh_own.at[i], dsem.at[sl, j])
-
-    def dh_other(i, sl, j):
-        return remote(stage.at[sl, half_rows(j, 1 - rg.k), :], dh_peer.at[i], dss.at[i], drs.at[i], rg.pt)
+    def dh_mine(i, sl, j, n):
+        ns = pl.ds(n * NC, NC)
+        return pltpu.make_async_copy(stage.at[sl, half_rows(j, rg.k), ns], dh_own.at[i, :, ns], dsem.at[sl, j, n])
+
+    def dh_other(i, sl, j, n):
+        ns = pl.ds(n * NC, NC)
+        return remote(stage.at[sl, half_rows(j, 1 - rg.k), ns], dh_peer.at[i, :, ns], dss.at[i, n], drs.at[i, n], rg.pt)
 
     def attn(i, j):
         q3 = q3_ref[i]
@@ -487,36 +493,39 @@
         tick(2)
         dqkv_ref[trow(ip, 2 * TILE), :] = dqkv_t[...]
 
-        @pl.when(it >= 2)
-        def _():
-            for j in range(2):
-                dh_mine(2 * (ip + 2) + j, sl, j).wait()
-                dh_other(2 * (ip + 2) + j, sl, j).wait_send()
         for n in range(4):
+            @pl.when(it >= 2)
+            def _():
+                for j in range(2):
+                    dh_mine(2 * (ip + 2) + j, sl, j, n).wait()
+                    dh_other(2 * (ip + 2) + j, sl, j, n).wait_send()
             ns = pl.ds(n * NC, NC)
             stage[sl, :, ns] = dot(dqkv_t[...], w_all[ns, :], NT).astype(BF16)
-            if n == 3:
-                for j in range(2):
-                    dh_mine(2 * ip + j, sl, j).start()
-                    dh_other(2 * ip + j, sl, j).start()
+            for j in range(2):
+                dh_mine(2 * ip + j, sl, j, n).start()
+                dh_other(2 * ip + j, sl, j, n).start()
             tick(3 + n)
 
+    gd.drain()
+    sc.drain(0, rg.nz - 1)
     for it in (np_ - 2, np_ - 1):
         ip = np_ - 1 - it
         for j in range(2):
-            dh_mine(2 * ip + j, it % 2, j).wait()
-            dh_other(2 * ip + j, it % 2, j).wait_send()
-    for i in range(nt):
-        dh_other(i, 0, 0).wait_recv()
-    sc.drain()
-    ga.drain()
-    gd.drain()
-
-
-def second_kernel(tp, dh_own, dh_peer, mix_own, mix_peer, part1_ref, x_ref, dy_ref, g_ref, h_full, dy_full, dqkv_ref, ot_ref,
+            for n in range(4):
+                dh_mine(2 * ip + j, it % 2, j, n).wait()
+                dh_other(2 * ip + j, it % 2, j, n).wait_send()
+
+    @pl.loop(0, nt)
+    def _(i):
+        for n in range(4):
+            dh_other(i, 0, 0, n).wait_recv()
+
+
+def second_kernel(tp, dh_own, dh_peer, mix_own, mix_peer, part1_ref, x_hbm, dy_hbm, g_ref, h_full, dy_full, dqkv_ref, ot_ref,
                   out_ref, gx_ref, dg_ref, dwq, dwk, dwv, dwo,
-                  ht, yt, skv, peer, dhr, part, slots, tot, hsem, ysem, pss, prs, gss, grs, bss, brs, *rsem):
+                  x_ref, dy_ref, xsem, ht, yt, skv, peer, dhr, part, slots, tot, hsem, ysem, pss, prs, gss, grs, bss, brs, *rsem):
     rg = Ring(tp)
+    rg.greet_all()
     rows, dm = x_ref.shape
     nz = rg.nz
     dq = dwq.shape[1]
@@ -547,8 +556,13 @@
 
     hload(0).start()
     yload(0).start()
-    rg.barrier_all()
+    xcp = [pltpu.make_async_copy(x_hbm, x_ref, xsem.at[0]), pltpu.make_async_copy(dy_hbm, dy_ref, xsem.at[1])]
+    for cp in xcp:
+        cp.start()
+    rg.met(tp - 1)
     sa.init()
+    for cp in xcp:
+        cp.wait()
     for d in range(2):
         out_ref[:, pl.ds(d * sb.H, done)] = part1_ref[d]
 
@@ -654,16 +668,27 @@
     for o in range(1, tp):
         bcast(o).start()
     dg_ref[:, gcol(rg.me)] = acc
+    sa.drain(0, nz - 1)
+    sb.drain(0, nz - 3)
+    for o in range(1, tp):
+        scat(o).wait_send()
     for s in rest[2:]:
         for u in range(SUBS):
             sb.tick(s, u)
     for o in range(1, tp):
         arrive(o).wait_recv()
     for o in range(1, tp):
-        scat(o).wait_send()
         bcast(o).wait_send()
-    sa.drain()
-    sb.drain()
+    sb.drain(nz - 3, nz - 1)
+
+
+def write_kernel(n, *refs):
+    sem = refs[-1]
+    cps = [pltpu.make_async_copy(refs[i], refs[n + i], sem.at[i]) for i in range(n)]
+    for cp in cps:
+        cp.start()
+    for cp in cps:
+        cp.wait()
 
 
 def solution(mesh):
@@ -696,33 +721,43 @@
         W2 = dm // 2 - W1
         h_full, dy_full, mix_own, mix_peer, dh_own, dh_peer, ot, dqkv, part1 = pl.pallas_call(
             functools.partial(first_kernel, tp, kvr),
-            out_shape=[full, full, blocks, blocks, blocks, blocks, sds((dq, seq), BF16), sds((seq, wd), BF16), sds((2, rows, W1), BF16)],
+            out_shape=[full, full, blocks, blocks, blocks, blocks, V((dq, seq), BF16), V((seq, wd), BF16), V((2, rows, W1), BF16)],
             in_specs=[VM, VM, VM, VM, ANY, ANY, ANY, ANY, ANY],
             out_specs=[ANY] * 6 + [VM] * 3,
             scratch_shapes=[V((rows, dm), BF16), V((dm, wd), BF16), V((dq, dm), BF16), V((2, 2 * TILE, dm), BF16), V((2, 2 * TILE, dm), BF16),
                             V((nt, qr, HEAD_DIM), BF16), V((seq, HEAD_DIM), BF16), V((seq, HEAD_DIM), BF16), V((HEAD_DIM, seq), BF16),
                             V((HEAD_DIM, seq), BF16), V((nt, 2, qr), F32), V((seq, HEAD_DIM), F32), V((seq, HEAD_DIM), F32), V((seq, TILE), F32),
                             V((nt, TILE), F32), V((seq, HEAD_DIM), F32), V((seq, HEAD_DIM), F32), V((2, qr, HEAD_DIM), BF16),
-                            V((2 * TILE, wd), BF16), DMA((4,)), DMA((2,)), DMA((2,)), DMA((nt,)), DMA((nt,)), DMA((2, 2)), DMA((nt,)), DMA((nt,))]
+                            V((2 * TILE, wd), BF16), DMA((4,)), DMA((2,)), DMA((2,)), DMA((nt,)), DMA((nt,)), DMA((2, 2, 4)), DMA((nt, 4)), DMA((nt, 4))]
             + Gather.scratch(tp) + Gather.scratch(tp) + Scatter.scratch(tp, rows, W1),
-            compiler_params=pltpu.CompilerParams(collective_id=1, has_side_effects=True, vmem_limit_bytes=VMEM_LIMIT),
+            compiler_params=pltpu.CompilerParams(collective_id=1, has_side_effects=True, vmem_limit_bytes=58 * 1024 * 1024),
             name="gather_attend_scatter",
         )(x, g2, pos2, frq, dy, wq, wk, wv, wo)
 
+        ot, dqkv, part1 = (pltpu.with_memory_space_constraint(a, pltpu.VMEM) for a in (ot, dqkv, part1))
         CB = dm // nz
-        out, grad_x, d_gain, d_wq, d_wk, d_wv, d_wo = pl.pallas_call(
+        res = pl.pallas_call(
             functools.partial(second_kernel, tp),
-            out_shape=[sds((rows, dm), BF16), sds((rows, dm), BF16), sds((1, dm), F32), V((dm, dq), BF16), V((dm, HEAD_DIM), F32),
+            out_shape=[V((rows, dm), BF16), V((rows, dm), BF16), V((1, dm), F32), V((dm, dq), BF16), V((dm, HEAD_DIM), F32),
                        V((dm, HEAD_DIM), F32), V((dq, dm), BF16)],
-            in_specs=[ANY, ANY, ANY, ANY, VM, VM, VM, VM, ANY, ANY, VM, VM],
+            in_specs=[ANY, ANY, ANY, ANY, VM, ANY, ANY, VM, ANY, ANY, VM, VM],
             out_specs=[VM] * 7,
-            scratch_shapes=[V((2, seq, CB), BF16), V((2, seq, CB), BF16), V((2, CB, 2 * HEAD_DIM), F32), V((nz, CB, 2 * HEAD_DIM), F32),
+            scratch_shapes=[V((rows, dm), BF16), V((rows, dm), BF16), DMA((2,)), V((2, seq, CB), BF16), V((2, seq, CB), BF16), V((2, CB, 2 * HEAD_DIM), F32), V((nz, CB, 2 * HEAD_DIM), F32),
                             V((rows, dm), BF16), V((1, dm), F32), V((tp, 1, dm // tp), F32), V((1, dm // tp), F32),
                             DMA((2,)), DMA((2,)), DMA((nz,)), DMA((nz,)), DMA((tp,)), DMA((tp,)), DMA((tp,)), DMA((tp,))]
             + Scatter.scratch(tp, rows, dm // 2) + Scatter.scratch(tp, rows, W2),
             compiler_params=pltpu.CompilerParams(collective_id=2, has_side_effects=True, vmem_limit_bytes=40 * 1024 * 1024),
             name="scatter_grads",
         )(dh_own, dh_peer, mix_own, mix_peer, part1, x, dy, g2, h_full, dy_full, dqkv, ot)
+        out, grad_x, d_gain, d_wq, d_wk, d_wv, d_wo = pl.pallas_call(
+            functools.partial(write_kernel, len(res)),
+            out_shape=[sds(r.shape, r.dtype) for r in res],
+            in_specs=[VM] * len(res),
+            out_specs=[ANY] * len(res),
+            scratch_shapes=[DMA((len(res),))],
+            compiler_params=pltpu.CompilerParams(vmem_limit_bytes=1024 * 1024),
+            name="write_results",
+        )(*res)
         return out, grad_x, d_wq, d_wk, d_wv, d_wo, d_gain.reshape(dm)
 
     specs_in = (P(('dp', 'tp'), None), P(('dp', 'tp'), None), P('dp'), P(), P(None, 'tp'), P(), P(), P('tp', None))

time: 286 us -> 276 us (0.965)
  local copies, waits for them, and re-layouts: 10.1 us -> 0 us
    unnamed x13 -> x0, local copies, waits for them, and re-layouts: 10.1 us -> none
    pallas_call x1, Pallas kernels: 181 us -> 177 us  [device_step(): pl.pallas_call(functools.partial(first_kernel, tp, kvr), out_shape=[full,...]
    pallas_call x1 -> x2, Pallas kernels: 93.8 us -> 97.3 us  [the longest x1 91 us: device_step(): pl.pallas_call(functools.partial(second_kernel, tp), out_shape=[V((rows,...]
where the time goes in v3:
time: 276 us; the launch traced here: 275 us
  Pallas kernels  274 us (99%)
    pallas_call x1, Pallas kernels, device_step(): pl.pallas_call(functools.partial(first_kernel, tp, kvr), out_shape=[full,...  177 us
    pallas_call x1, Pallas kernels, device_step(): pl.pallas_call(functools.partial(second_kernel, tp), out_shape=[V((rows,...  91 us
    pallas_call x1, Pallas kernels, device_step(): pl.pallas_call(functools.partial(write_kernel, len(res)), out_shape=[sds(...  6.22 us

profile of v3, /device:TPU:21, one launch (start us, length us, event | category | flops | bytes accessed | tf_op | source)
XLA Modules:
  0.0 275.0 jit_solution(14260305548712877120)
XLA Ops:
  0.6 176.9 %gather_attend_scatter.1 = (bf16[1024,6144]{1,0:T(8,128)(2,1)}, bf16[1024,6144]{1,0:T(8,128)(2,1)}, bf16[8,64,6144]{2,1,0:T(8,128)(2,1)}, bf16[8,64,6144]{2,1,0:...) custom-call(bf16[64,6144]{1,0:T(8,128)(2,1)} %x_hbm.1, ...), custom_call_target="tpu_custom_call" | custom-call | tf_op jit(solution)/shard_map/gather_attend_scatter/pallas_call | solution.py:722
  177.6 91.0 %scatter_grads.1 = (bf16[64,6144]{1,0:T(8,128)(2,1)S(1)}, bf16[64,6144]{1,0:T(8,128)(2,1)S(1)}, f32[1,6144]{1,0:T(1,128)S(1)}, bf16[6144,384]{1,0:T(8,128)(2,1)S...) custom-call(bf16[8,64,6144]{2,1,0:T(8,128)(2,1)} %get-tuple-element.30.dh_own, ...), custom_call_target="tpu_custom_call" | custom-call | tf_op jit(solution)/shard_map/scatter_grads/pallas_call | solution.py:739
  268.6 6.2 %write_results.1 = (bf16[64,6144]{1,0:T(8,128)(2,1)}, bf16[64,6144]{1,0:T(8,128)(2,1)}, f32[1,6144]{1,0:T(1,128)}, bf16[6144,384]{1,0:T(8,128)(2,1)}, f32[6144,1...) custom-call(bf16[64,6144]{1,0:T(8,128)(2,1)S(1)} %get-tuple-element.39.refs_0_, ...), custom_call_target="tpu_custom_call" | custom-call | tf_op jit(solution)/shard_map/write_results/pallas_call | solution.py:752

commit v4 on v3

--- a/solution.py
+++ b/solution.py
@@ -61,10 +61,14 @@
     return pltpu.make_async_remote_copy(src, dst, ss, rs, device_id={"tp": dev}, device_id_type=MESH)
 
 
+def wait_bytes(ref, sem):
+    pltpu.make_async_copy(ref, ref, sem).wait()
+
+
 class Gather:
-    def __init__(self, rg, src, dst, rows, ss, rs, dss, drs, ls):
+    def __init__(self, rg, src, dst, rows, ss, rs, drs, ls):
         self.rg, self.src, self.dst, self.R = rg, src, dst, rows
-        self.ss, self.rs, self.dss, self.drs, self.ls = ss, rs, dss, drs, ls
+        self.ss, self.rs, self.drs, self.ls = ss, rs, drs, ls
         self.H = rows // 2
         self.steps = rg.nz - 1
 
@@ -84,27 +88,28 @@
     def own(self, d, s):
         h = self.half(d, s)
         return remote(self.src.at[pl.ds(h * self.H, self.H), :], self.dst.at[self.rows(self.rg.c, self.rg.k, h), :],
-                      self.ss.at[d, s], self.rs.at[d, s], self.dev(d))
+                      self.ss, self.rs.at[d, s], self.dev(d))
 
     def recv_rows(self, d, s, core):
         return self.rows(self.origin(d, s), core, self.half(d, s))
 
     def fwd(self, d, s):
         r = self.recv_rows(d, s - 2, self.rg.k)
-        return remote(self.dst.at[r, :], self.dst.at[r, :], self.ss.at[d, s], self.rs.at[d, s], self.dev(d))
+        return remote(self.dst.at[r, :], self.dst.at[r, :], self.ss, self.rs.at[d, s], self.dev(d))
 
     def recv(self, d, s):
         r = self.recv_rows(d, s, self.rg.k)
-        return remote(self.dst.at[r, :], self.dst.at[r, :], self.ss.at[d, s], self.rs.at[d, s], self.dev(d))
-
-    def pair(self, i, r):
-        return remote(self.dst.at[r, :], self.dst.at[r, :], self.dss.at[i], self.drs.at[i], self.rg.pt)
+        return remote(self.dst.at[r, :], self.dst.at[r, :], self.ss, self.rs.at[d, s], self.dev(d))
+
+    def pair(self, d, s):
+        r = self.recv_rows(d, s, self.rg.k)
+        return remote(self.dst.at[r, :], self.dst.at[r, :], self.ss, self.drs.at[s // 2], self.rg.pt)
 
     def block(self, dev):
         return pl.ds(pl.multiple_of(dev * self.R, self.R), self.R)
 
     def pair_own(self):
-        return remote(self.src, self.dst.at[self.block(self.rg.me), :], self.dss.at[0], self.drs.at[0], self.rg.pt)
+        return remote(self.src, self.dst.at[self.block(self.rg.me), :], self.ss, self.drs.at[0], self.rg.pt)
 
     def local(self):
         return pltpu.make_async_copy(self.src, self.dst.at[self.block(self.rg.me), :], self.ls)
@@ -117,40 +122,31 @@
         self.local().start()
         self.pair_own().start()
 
-    def tick(self, s, forward=True):
+    def tick(self, s):
         for d in range(2):
             self.recv(d, s).wait_recv()
-            if isinstance(s, int):
-                if s + 2 < self.steps:
-                    self.fwd(d, s + 2).start()
-            else:
-                @pl.when(s + 2 < self.steps)
-                def _():
-                    self.fwd(d, s + 2).start()
-            self.pair(1 + 2 * s + d, self.recv_rows(d, s, self.rg.k)).start()
-
-    def wait_pair(self):
-        self.local().wait()
-        self.pair(0, self.block(self.rg.pt)).wait_recv()
-        for s in range(self.steps):
-            for d in range(2):
-                self.pair(1 + 2 * s + d, self.recv_rows(d, s, 1 - self.rg.k)).wait_recv()
+            if s + 2 < self.steps:
+                self.fwd(d, s + 2).start()
+            self.pair(d, s).start()
+
+    def wait_pair(self, g):
+        n = 2 * self.H * min(2, self.steps - 2 * g)
+        if g == 0:
+            self.local().wait()
+            n += self.R
+        wait_bytes(self.dst.at[pl.ds(0, n), :], self.drs.at[g])
+
+    def groups(self):
+        return (self.steps + 1) // 2
 
     def drain(self):
-        self.pair_own().wait_send()
-        for s in range(self.steps):
-            for d in range(2):
-                self.pair(1 + 2 * s + d, self.recv_rows(d, s, self.rg.k)).wait_send()
-                if s < 2:
-                    self.own(d, s).wait_send()
-                else:
-                    self.fwd(d, s).wait_send()
+        wait_bytes(self.dst.at[pl.ds(0, self.R + 4 * self.H * self.steps), :], self.ss)
 
     @staticmethod
     def scratch(tp):
         n = tp // 2 - 1
         dma = pltpu.SemaphoreType.DMA
-        return [dma((2, n)), dma((2, n)), dma((1 + 2 * n,)), dma((1 + 2 * n,)), dma]
+        return [dma, dma((2, n)), dma(((n + 1) // 2,)), dma]
 
 
 class Scatter:
@@ -180,7 +176,7 @@
                 self.load(w, d, s).wait()
 
     def send(self, d, u, s):
-        return remote(self.buf.at[d, u, s], self.buf.at[d, u, s + 1], self.ss.at[d, u, s], self.rs.at[d, u, s],
+        return remote(self.buf.at[d, u, s], self.buf.at[d, u, s + 1], self.ss, self.rs.at[d, u, s],
                       self.rg.up if d == 0 else self.rg.dn)
 
     def cols(self, u):
@@ -225,19 +221,15 @@
             def _():
                 self.final(d, u, self.mine(d, s, u) + self.buf[d, u, s].astype(F32))
 
-    def drain(self, lo, hi):
-        @pl.loop(lo, hi)
-        def _(s):
-            for d in range(2):
-                for u in range(SUBS):
-                    self.send(d, u, s).wait_send()
+    def drain(self):
+        wait_bytes(self.buf.at[:, :, pl.ds(0, self.rg.nz - 1)], self.ss)
 
     @staticmethod
     def scratch(tp, rows, W):
         nz = tp // 2
         dma = pltpu.SemaphoreType.DMA
         return [pltpu.VMEM((2, 2, 2, rows, W), BF16), dma((2, 2, 2)), pltpu.VMEM((2, SUBS, nz, rows, W // SUBS), BF16),
-                dma((2, SUBS, nz - 1)), dma((2, SUBS, nz - 1))]
+                dma, dma((2, SUBS, nz - 1))]
 
 
 def weight_copies(kv, wq, wk, wv, wo, w_all, wo_v, sem):
@@ -271,11 +263,14 @@
     return (key <= qry) & (kdc == kdr)
 
 
-def first_kernel(tp, kvr, x_ref, g_ref, pos_ref, frq_ref, dy_ref, wq, wk, wv, wo,
+def first_kernel(tp, kvr, x_hbm, g_ref, pos_ref, frq_ref, dy_ref, wq, wk, wv, wo,
                  h_full, dy_full, mix_own, mix_peer, dh_own, dh_peer, ot_ref, dqkv_ref, out_ref,
-                 hown, w_all, wo_v, tile, stage, q3_ref, k_ref, v_ref, vt, kt, st_ref, cos_ref, sin_ref, kdc_ref, kdr_ref,
-                 dk_acc, dv_acc, do3, dqkv_t, wsem, tsem, msem, mss, mrs, dsem, dss, drs, *sems):
+                 x_ref, hown, w_all, wo_v, tile, stage, q3_ref, k_ref, v_ref, vt, kt, st_ref, cos_ref, sin_ref, kdc_ref, kdr_ref,
+                 dk_acc, dv_acc, do3, dqkv_t, xsem, wsem, tsem, ysem, msem, mss, mrs, dsem, dss, drs, *sems):
     rg = Ring(tp)
+    rg.greet_near()
+    xcp = pltpu.make_async_copy(x_hbm, x_ref, xsem)
+    xcp.start()
     rows, dm = x_ref.shape
     seq = rows * tp
     nt = seq // TILE
@@ -283,19 +278,19 @@
     dq = wq.shape[1]
     nh = dq // HEAD_DIM
     half = TILE // 2
-    ga = Gather(rg, hown, h_full, rows, *sems[:5])
-    gd = Gather(rg, dy_ref, dy_full, rows, *sems[5:10])
+    ga = Gather(rg, hown, h_full, rows, *sems[:4])
+    gd = Gather(rg, dy_ref, dy_full, rows, *sems[4:8])
 
     def final(d, u, val):
         xs = pl.ds(pl.multiple_of(d * sc.H + u * sc.CW, sc.CW), sc.CW)
         out_ref[d, :, sc.cols(u)] = (x_ref[:, xs].astype(F32) + val).astype(BF16)
 
-    sc = Scatter(rg, mix_own, mix_peer, 0, *sems[10:], final)
-    rg.greet_near()
+    sc = Scatter(rg, mix_own, mix_peer, 0, *sems[8:], final)
     wcp = weight_copies(rg.me // kvr, wq, wk, wv, wo, w_all, wo_v, wsem)
     for cp in wcp:
         cp.start()
     RB = 16
+    xcp.wait()
 
     @pl.loop(0, rows // RB)
     def _(r):
@@ -326,7 +321,8 @@
         ga.tick(s)
         if s >= ga.steps - 2:
             gd.start_ring(s - (ga.steps - 2))
-    ga.wait_pair()
+    for n in range(ga.groups()):
+        ga.wait_pair(n)
     for cp in wcp:
         cp.wait()
 
@@ -370,7 +366,7 @@
         return pltpu.make_async_copy(stage.at[i % 2, half_rows(0, rg.k), :], mix_own.at[i], msem.at[i % 2])
 
     def mix_other(i):
-        return remote(stage.at[i % 2, half_rows(0, 1 - rg.k), :], mix_peer.at[i], mss.at[i], mrs.at[i], rg.pt)
+        return remote(stage.at[i % 2, half_rows(0, 1 - rg.k), :], mix_peer.at[i], mss.at[i % 2], mrs, rg.pt)
 
     NC = dm // 4
 
@@ -413,19 +409,47 @@
     for i in (nt - 2, nt - 1):
         mix_mine(i).wait()
         mix_other(i).wait_send()
-    for i in range(nt):
-        mix_other(i).wait_recv()
+    wait_bytes(mix_peer, mrs)
     sc.start_loads(0)
-    for s in range(3, gd.steps - 2):
-        gd.tick(s)
+
+    def yload(chip, sl, j):
+        return pltpu.make_async_copy(dy_full.at[trow(rg.chip(chip)), :], tile.at[sl, pl.ds(j * TILE, TILE), :], ysem.at[sl, j])
+
+    def pair_of(g):
+        return (rg.c + g + 1, rg.c - g - 1) if g + 1 < np_ else (rg.c + np_, rg.c)
+
+    def start_y(g, js=(0, 1)):
+        for j in js:
+            yload(pair_of(g)[j], g % 2, j).start()
+
+    def d_o(g):
+        for j in range(2):
+            yload(pair_of(g)[j], g % 2, j).wait()
+        do = dot(tile[g % 2], wo_v[...], NT).astype(BF16)
+        for j in range(2):
+            t = rg.chip(pair_of(g)[j])
+            for h in range(nh):
+                do3[t, pl.ds(h * TILE, TILE), :] = do[j * TILE:(j + 1) * TILE, h * HEAD_DIM:(h + 1) * HEAD_DIM]
+
+    gd.tick(3)
+    gd.wait_pair(0)
+    gd.wait_pair(1)
+    start_y(0)
+    start_y(1)
+    gd.tick(4)
     sc.init()
     ga.drain()
-    for s in range(max(3, gd.steps - 2), gd.steps):
-        gd.tick(s)
-    gd.wait_pair()
-
-    def yload(it):
-        return pltpu.make_async_copy(dy_full.at[trow(np_ - 1 - it, 2 * TILE), :], tile.at[it % 2], tsem.at[it % 2])
+    d_o(0)
+    d_o(1)
+    start_y(3, (1,))
+    gd.tick(5)
+    gd.wait_pair(2)
+    start_y(2)
+    d_o(2)
+    gd.tick(6)
+    gd.wait_pair(3)
+    start_y(3, (0,))
+    d_o(3)
 
     def dh_mine(i, sl, j, n):
         ns = pl.ds(n * NC, NC)
@@ -433,11 +457,11 @@
 
     def dh_other(i, sl, j, n):
         ns = pl.ds(n * NC, NC)
-        return remote(stage.at[sl, half_rows(j, 1 - rg.k), ns], dh_peer.at[i, :, ns], dss.at[i, n], drs.at[i, n], rg.pt)
+        return remote(stage.at[sl, half_rows(j, 1 - rg.k), ns], dh_peer.at[i, :, ns], dss.at[sl, j, n], drs, rg.pt)
 
     def attn(i, j):
         q3 = q3_ref[i]
-        do = do3[j]
+        do = do3[i]
         s = dot(k_ref[...], q3, NT) * SCORE_SCALE
         keep = keep_t(kdc_ref[...], kdr_ref[pl.ds(i, 1), :], i, seq)
         dp = dot(v_ref[...], do, NT)
@@ -465,27 +489,17 @@
         dqkv_t[jr, pl.ds(dq, HEAD_DIM)] = rope_t(t, cos, sin).astype(BF16)
         dqkv_t[jr, pl.ds(dq + HEAD_DIM, HEAD_DIM)] = dv_acc[trow(i), :].astype(BF16)
 
-    yload(0).start()
     per = -(-SUBS * (rg.nz - 1) // np_)
 
     @pl.loop(0, np_)
     def _(it):
         ip = np_ - 1 - it
         sl = it % 2
-        yload(it).wait()
-
-        @pl.when(it + 1 < np_)
-        def _():
-            yload(it + 1).start()
 
         def tick(n):
             at = per * it + n
             sc.tick(1 + at // SUBS, at % SUBS)
 
-        do = dot(tile[sl], wo_v[...], NT).astype(BF16)
-        for j in range(2):
-            for h in range(nh):
-                do3[j, pl.ds(h * TILE, TILE), :] = do[j * TILE:(j + 1) * TILE, h * HEAD_DIM:(h + 1) * HEAD_DIM]
         tick(0)
         attn(2 * ip + 1, 1)
         tick(1)
@@ -507,7 +521,7 @@
             tick(3 + n)
 
     gd.drain()
-    sc.drain(0, rg.nz - 1)
+    sc.drain()
     for it in (np_ - 2, np_ - 1):
         ip = np_ - 1 - it
         for j in range(2):
@@ -515,10 +529,7 @@
                 dh_mine(2 * ip + j, it % 2, j, n).wait()
                 dh_other(2 * ip + j, it % 2, j, n).wait_send()
 
-    @pl.loop(0, nt)
-    def _(i):
-        for n in range(4):
-            dh_other(i, 0, 0, n).wait_recv()
+    wait_bytes(dh_peer, drs)
 
 
 def second_kernel(tp, dh_own, dh_peer, mix_own, mix_peer, part1_ref, x_hbm, dy_hbm, g_ref, h_full, dy_full, dqkv_ref, ot_ref,
@@ -530,7 +541,7 @@
     nz = rg.nz
     dq = dwq.shape[1]
     CB = dm // nz
-    LAG = 5
+    LAG = 4
     done = part1_ref.shape[-1]
 
     def final_a(d, u, val):
@@ -567,7 +578,7 @@
         out_ref[:, pl.ds(d * sb.H, done)] = part1_ref[d]
 
     def to_peer(it):
-        return remote(skv.at[it % 2], peer.at[it], pss.at[it], prs.at[it], rg.pt)
+        return remote(skv.at[it % 2], peer.at[it], pss.at[it % 2], prs.at[it], rg.pt)
 
     def pair_sum(it):
         to_peer(it).wait_recv()
@@ -617,8 +628,6 @@
         def _():
             pair_sum(it - 1)
 
-    for u in range(SUBS):
-        sb.tick(nz - LAG, u)
     RB = 16
     part[...] = jnp.zeros_like(part)
 
@@ -643,43 +652,35 @@
         return lax.rem(rg.me + o, tp)
 
     def scat(o):
-        return remote(part.at[:, gcol(dev(o))], slots.at[o], gss.at[o], grs.at[o], dev(o))
+        return remote(part.at[:, gcol(dev(o))], slots.at[o], gss, grs, dev(o))
 
     for o in range(1, tp):
         scat(o).start()
     pair_sum(nz - 1)
-    rest = list(range(nz - LAG + 1, nz))
+    rest = list(range(nz - LAG, nz))
     for s in rest[:2]:
         for u in range(SUBS):
             sb.tick(s, u)
     acc = part[:, gcol(rg.me)]
+    wait_bytes(slots.at[pl.ds(1, tp - 1)], grs)
     for o in range(1, tp):
-        scat(o).wait_recv()
         acc = acc + slots[o]
     tot[...] = acc
 
     def bcast(o):
-        return remote(tot, dg_ref.at[:, gcol(rg.me)], bss.at[o], brs.at[o], dev(o))
-
-    def arrive(o):
-        src = lax.rem(rg.me + tp - o, tp)
-        return remote(tot, dg_ref.at[:, gcol(src)], bss.at[o], brs.at[o], dev(o))
+        return remote(tot, dg_ref.at[:, gcol(rg.me)], bss, brs, dev(o))
 
     for o in range(1, tp):
         bcast(o).start()
     dg_ref[:, gcol(rg.me)] = acc
-    sa.drain(0, nz - 1)
-    sb.drain(0, nz - 3)
-    for o in range(1, tp):
-        scat(o).wait_send()
+    sa.drain()
+    wait_bytes(slots.at[pl.ds(1, tp - 1)], gss)
     for s in rest[2:]:
         for u in range(SUBS):
             sb.tick(s, u)
-    for o in range(1, tp):
-        arrive(o).wait_recv()
-    for o in range(1, tp):
-        bcast(o).wait_send()
-    sb.drain(nz - 3, nz - 1)
+    wait_bytes(slots.at[pl.ds(1, tp - 1)], brs)
+    wait_bytes(slots.at[pl.ds(1, tp - 1)], bss)
+    sb.drain()
 
 
 def write_kernel(n, *refs):
@@ -722,13 +723,13 @@
         h_full, dy_full, mix_own, mix_peer, dh_own, dh_peer, ot, dqkv, part1 = pl.pallas_call(
             functools.partial(first_kernel, tp, kvr),
             out_shape=[full, full, blocks, blocks, blocks, blocks, V((dq, seq), BF16), V((seq, wd), BF16), V((2, rows, W1), BF16)],
-            in_specs=[VM, VM, VM, VM, ANY, ANY, ANY, ANY, ANY],
+            in_specs=[ANY, VM, VM, VM, ANY, ANY, ANY, ANY, ANY],
             out_specs=[ANY] * 6 + [VM] * 3,
-            scratch_shapes=[V((rows, dm), BF16), V((dm, wd), BF16), V((dq, dm), BF16), V((2, 2 * TILE, dm), BF16), V((2, 2 * TILE, dm), BF16),
+            scratch_shapes=[V((rows, dm), BF16), V((rows, dm), BF16), V((dm, wd), BF16), V((dq, dm), BF16), V((2, 2 * TILE, dm), BF16), V((2, 2 * TILE, dm), BF16),
                             V((nt, qr, HEAD_DIM), BF16), V((seq, HEAD_DIM), BF16), V((seq, HEAD_DIM), BF16), V((HEAD_DIM, seq), BF16),
                             V((HEAD_DIM, seq), BF16), V((nt, 2, qr), F32), V((seq, HEAD_DIM), F32), V((seq, HEAD_DIM), F32), V((seq, TILE), F32),
-                            V((nt, TILE), F32), V((seq, HEAD_DIM), F32), V((seq, HEAD_DIM), F32), V((2, qr, HEAD_DIM), BF16),
-                            V((2 * TILE, wd), BF16), DMA((4,)), DMA((2,)), DMA((2,)), DMA((nt,)), DMA((nt,)), DMA((2, 2, 4)), DMA((nt, 4)), DMA((nt, 4))]
+                            V((nt, TILE), F32), V((seq, HEAD_DIM), F32), V((seq, HEAD_DIM), F32), V((nt, qr, HEAD_DIM), BF16),
+                            V((2 * TILE, wd), BF16), DMA, DMA((4,)), DMA((2,)), DMA((2, 2)), DMA((2,)), DMA((2,)), DMA, DMA((2, 2, 4)), DMA((2, 2, 4)), DMA]
             + Gather.scratch(tp) + Gather.scratch(tp) + Scatter.scratch(tp, rows, W1),
             compiler_params=pltpu.CompilerParams(collective_id=1, has_side_effects=True, vmem_limit_bytes=58 * 1024 * 1024),
             name="gather_attend_scatter",
@@ -744,7 +745,7 @@
             out_specs=[VM] * 7,
             scratch_shapes=[V((rows, dm), BF16), V((rows, dm), BF16), DMA((2,)), V((2, seq, CB), BF16), V((2, seq, CB), BF16), V((2, CB, 2 * HEAD_DIM), F32), V((nz, CB, 2 * HEAD_DIM), F32),
                             V((rows, dm), BF16), V((1, dm), F32), V((tp, 1, dm // tp), F32), V((1, dm // tp), F32),
-                            DMA((2,)), DMA((2,)), DMA((nz,)), DMA((nz,)), DMA((tp,)), DMA((tp,)), DMA((tp,)), DMA((tp,))]
+                            DMA((2,)), DMA((2,)), DMA((2,)), DMA((nz,)), DMA, DMA, DMA, DMA]
             + Scatter.scratch(tp, rows, dm // 2) + Scatter.scratch(tp, rows, W2),
             compiler_params=pltpu.CompilerParams(collective_id=2, has_side_effects=True, vmem_limit_bytes=40 * 1024 * 1024),
             name="scatter_grads",

time: 276 us -> 276 us (level)
  no operation moved by 1% of the time
where the time goes in v4:
time: 276 us; the launch traced here: 275 us
  Pallas kernels  274 us (99%)
    pallas_call x1, Pallas kernels, device_step(): pl.pallas_call(functools.partial(first_kernel, tp, kvr), out_shape=[full,...  178 us
    pallas_call x1, Pallas kernels, device_step(): pl.pallas_call(functools.partial(second_kernel, tp), out_shape=[V((rows,...  90.2 us
    pallas_call x1, Pallas kernels, device_step(): pl.pallas_call(functools.partial(write_kernel, len(res)), out_shape=[sds(...  6.22 us

profile of v4, /device:TPU:21, one launch (start us, length us, event | category | flops | bytes accessed | tf_op | source)
XLA Modules:
  0.0 275.0 jit_solution(7546926120831859992)
XLA Ops:
  0.6 177.8 %gather_attend_scatter.1 = (bf16[1024,6144]{1,0:T(8,128)(2,1)}, bf16[1024,6144]{1,0:T(8,128)(2,1)}, bf16[8,64,6144]{2,1,0:T(8,128)(2,1)}, bf16[8,64,6144]{2,1,0:...) custom-call(bf16[64,6144]{1,0:T(8,128)(2,1)} %x_hbm.3, ...), custom_call_target="tpu_custom_call" | custom-call | tf_op jit(solution)/shard_map/gather_attend_scatter/pallas_call | solution.py:723
  178.4 90.2 %scatter_grads.1 = (bf16[64,6144]{1,0:T(8,128)(2,1)S(1)}, bf16[64,6144]{1,0:T(8,128)(2,1)S(1)}, f32[1,6144]{1,0:T(1,128)S(1)}, bf16[6144,384]{1,0:T(8,128)(2,1)S...) custom-call(bf16[8,64,6144]{2,1,0:T(8,128)(2,1)} %get-tuple-element.30.dh_own, ...), custom_call_target="tpu_custom_call" | custom-call | tf_op jit(solution)/shard_map/scatter_grads/pallas_call | solution.py:740
  268.6 6.2 %write_results.1 = (bf16[64,6144]{1,0:T(8,128)(2,1)}, bf16[64,6144]{1,0:T(8,128)(2,1)}, f32[1,6144]{1,0:T(1,128)}, bf16[6144,384]{1,0:T(8,128)(2,1)}, f32[6144,1...) custom-call(bf16[64,6144]{1,0:T(8,128)(2,1)S(1)} %get-tuple-element.39.refs_0_, ...), custom_call_target="tpu_custom_call" | custom-call | tf_op jit(solution)/shard_map/write_results/pallas_call | solution.py:753

commit v5 on v4

--- a/solution.py
+++ b/solution.py
@@ -287,8 +287,6 @@
 
     sc = Scatter(rg, mix_own, mix_peer, 0, *sems[8:], final)
     wcp = weight_copies(rg.me // kvr, wq, wk, wv, wo, w_all, wo_v, wsem)
-    for cp in wcp:
-        cp.start()
     RB = 16
     xcp.wait()
 
@@ -303,6 +301,8 @@
     ga.start_ring(1)
     ga.start_local()
     gd.start_local()
+    for cp in wcp:
+        cp.start()
     lane = lax.broadcasted_iota(jnp.int32, (TILE, TILE), 1)
     sgn = jnp.where(lane < HEAD_DIM // 2, -1.0, 1.0).astype(F32)
     kdr_ref[...] = (pos_ref[...] - (lax.broadcasted_iota(jnp.int32, pos_ref.shape, 0) * TILE
@@ -422,7 +422,9 @@
         for j in js:
             yload(pair_of(g)[j], g % 2, j).start()
 
-    def d_o(g):
+    def d_o(g, meanwhile=None):
+        if meanwhile is not None:
+            meanwhile()
         for j in range(2):
             yload(pair_of(g)[j], g % 2, j).wait()
         do = dot(tile[g % 2], wo_v[...], NT).astype(BF16)
@@ -449,7 +451,7 @@
     gd.tick(6)
     gd.wait_pair(3)
     start_y(3, (0,))
-    d_o(3)
+    d_o(3, lambda: sc.tick(jnp.int32(1), 0))
 
     def dh_mine(i, sl, j, n):
         ns = pl.ds(n * NC, NC)
@@ -489,7 +491,8 @@
         dqkv_t[jr, pl.ds(dq, HEAD_DIM)] = rope_t(t, cos, sin).astype(BF16)
         dqkv_t[jr, pl.ds(dq + HEAD_DIM, HEAD_DIM)] = dv_acc[trow(i), :].astype(BF16)
 
-    per = -(-SUBS * (rg.nz - 1) // np_)
+    per = 6
+    ticks = SUBS * (rg.nz - 1)
 
     @pl.loop(0, np_)
     def _(it):
@@ -497,7 +500,7 @@
         sl = it % 2
 
         def tick(n):
-            at = per * it + n
+            at = 1 + per * it + n
             sc.tick(1 + at // SUBS, at % SUBS)
 
         tick(0)
@@ -518,8 +521,12 @@
             for j in range(2):
                 dh_mine(2 * ip + j, sl, j, n).start()
                 dh_other(2 * ip + j, sl, j, n).start()
-            tick(3 + n)
-
+            if n < 3:
+                tick(3 + n)
+
+    @pl.loop(1 + per * np_, ticks)
+    def _(at):
+        sc.tick(1 + at // SUBS, at % SUBS)
     gd.drain()
     sc.drain()
     for it in (np_ - 2, np_ - 1):
@@ -541,7 +548,7 @@
     nz = rg.nz
     dq = dwq.shape[1]
     CB = dm // nz
-    LAG = 4
+    LAG = 3
     done = part1_ref.shape[-1]
 
     def final_a(d, u, val):
@@ -658,7 +665,7 @@
         scat(o).start()
     pair_sum(nz - 1)
     rest = list(range(nz - LAG, nz))
-    for s in rest[:2]:
+    for s in rest[:-2]:
         for u in range(SUBS):
             sb.tick(s, u)
     acc = part[:, gcol(rg.me)]
@@ -675,7 +682,7 @@
     dg_ref[:, gcol(rg.me)] = acc
     sa.drain()
     wait_bytes(slots.at[pl.ds(1, tp - 1)], gss)
-    for s in rest[2:]:
+    for s in rest[-2:]:
         for u in range(SUBS):
             sb.tick(s, u)
     wait_bytes(slots.at[pl.ds(1, tp - 1)], brs)

time: 276 us -> 270 us (0.978)
  Pallas kernels: 274 us -> 269 us
    pallas_call x1, Pallas kernels: 178 us -> 171 us  [device_step(): pl.pallas_call(functools.partial(first_kernel, tp, kvr), out_shape=[full,...]
where the time goes in v5:
time: 270 us
  Pallas kernels  269 us (100%)
    pallas_call x1, Pallas kernels, device_step(): pl.pallas_call(functools.partial(first_kernel, tp, kvr), out_shape=[full,...  171 us
    pallas_call x1, Pallas kernels, device_step(): pl.pallas_call(functools.partial(second_kernel, tp), out_shape=[V((rows,...  91.1 us
    pallas_call x1, Pallas kernels, device_step(): pl.pallas_call(functools.partial(write_kernel, len(res)), out_shape=[sds(...  6.22 us

profile of v5, /device:TPU:21, one launch (start us, length us, event | category | flops | bytes accessed | tf_op | source)
XLA Modules:
  0.0 269.6 jit_solution(6436329218521694432)
XLA Ops:
  0.6 171.5 %gather_attend_scatter.1 = (bf16[1024,6144]{1,0:T(8,128)(2,1)}, bf16[1024,6144]{1,0:T(8,128)(2,1)}, bf16[8,64,6144]{2,1,0:T(8,128)(2,1)}, bf16[8,64,6144]{2,1,0:...) custom-call(bf16[64,6144]{1,0:T(8,128)(2,1)} %x_hbm.3, ...), custom_call_target="tpu_custom_call" | custom-call | tf_op jit(solution)/shard_map/gather_attend_scatter/pallas_call | solution.py:730
  172.1 91.1 %scatter_grads.1 = (bf16[64,6144]{1,0:T(8,128)(2,1)S(1)}, bf16[64,6144]{1,0:T(8,128)(2,1)S(1)}, f32[1,6144]{1,0:T(1,128)S(1)}, bf16[6144,384]{1,0:T(8,128)(2,1)S...) custom-call(bf16[8,64,6144]{2,1,0:T(8,128)(2,1)} %get-tuple-element.30.dh_own, ...), custom_call_target="tpu_custom_call" | custom-call | tf_op jit(solution)/shard_map/scatter_grads/pallas_call | solution.py:747
  263.2 6.2 %write_results.1 = (bf16[64,6144]{1,0:T(8,128)(2,1)}, bf16[64,6144]{1,0:T(8,128)(2,1)}, f32[1,6144]{1,0:T(1,128)}, bf16[6144,384]{1,0:T(8,128)(2,1)}, f32[6144,1...) custom-call(bf16[64,6144]{1,0:T(8,128)(2,1)S(1)} %get-tuple-element.39.refs_0_, ...), custom_call_target="tpu_custom_call" | custom-call | tf_op jit(solution)/shard_map/write_results/pallas_call | solution.py:760

commit v6 on v5

--- a/solution.py
+++ b/solution.py
@@ -46,9 +46,6 @@
 
     def greet_near(self):
         self.greet((self.up, self.dn, self.pt))
-
-    def greet_all(self):
-        self.greet([lax.rem(self.me + o, self.tp) for o in range(1, self.tp)])
 
     def met(self, count):
         pl.semaphore_wait(pltpu.get_barrier_semaphore(), count)
@@ -543,7 +540,7 @@
                   out_ref, gx_ref, dg_ref, dwq, dwk, dwv, dwo,
                   x_ref, dy_ref, xsem, ht, yt, skv, peer, dhr, part, slots, tot, hsem, ysem, pss, prs, gss, grs, bss, brs, *rsem):
     rg = Ring(tp)
-    rg.greet_all()
+    rg.greet_near()
     rows, dm = x_ref.shape
     nz = rg.nz
     dq = dwq.shape[1]
@@ -577,7 +574,7 @@
     xcp = [pltpu.make_async_copy(x_hbm, x_ref, xsem.at[0]), pltpu.make_async_copy(dy_hbm, dy_ref, xsem.at[1])]
     for cp in xcp:
         cp.start()
-    rg.met(tp - 1)
+    rg.met(3)
     sa.init()
     for cp in xcp:
         cp.wait()
@@ -638,31 +635,38 @@
     RB = 16
     part[...] = jnp.zeros_like(part)
 
+    def normed(rr):
+        xf = x_ref[rr, :].astype(F32)
+        inv = lax.rsqrt(jnp.mean(xf * xf, axis=-1, keepdims=True) + NORM_EPS)
+        return xf * inv, inv
+
     @pl.loop(0, rows // RB)
     def _(r):
         rr = trow(r, RB)
-        xf = x_ref[rr, :].astype(F32)
-        inv = lax.rsqrt(jnp.mean(xf * xf, axis=-1, keepdims=True) + NORM_EPS)
-        xh = xf * inv
-        dh = dhr[rr, :].astype(F32)
-        part[...] += jnp.sum(dh * xh, axis=0, keepdims=True)
-        a = dh * g_ref[...]
+        part[...] += jnp.sum(dhr[rr, :].astype(F32) * normed(rr)[0], axis=0, keepdims=True)
+
+    GW = dm // tp
+
+    def gcol(dev):
+        return pl.ds(pl.multiple_of(dev * GW, GW), GW)
+
+    def dev(o):
+        return lax.rem(rg.me + o, tp)
+
+    def scat(o):
+        return remote(part.at[:, gcol(dev(o))], slots.at[o], gss, grs, dev(o))
+
+    for o in range(1, tp):
+        scat(o).start()
+
+    @pl.loop(0, rows // RB)
+    def _(r):
+        rr = trow(r, RB)
+        xh, inv = normed(rr)
+        a = dhr[rr, :].astype(F32) * g_ref[...]
         di = inv * (a - xh * jnp.mean(a * xh, axis=-1, keepdims=True))
         gx_ref[rr, :] = (dy_ref[rr, :].astype(F32) + di).astype(BF16)
 
-    GW = dm // tp
-
-    def gcol(dev):
-        return pl.ds(pl.multiple_of(dev * GW, GW), GW)
-
-    def dev(o):
-        return lax.rem(rg.me + o, tp)
-
-    def scat(o):
-        return remote(part.at[:, gcol(dev(o))], slots.at[o], gss, grs, dev(o))
-
-    for o in range(1, tp):
-        scat(o).start()
     pair_sum(nz - 1)
     rest = list(range(nz - LAG, nz))
     for s in rest[:-2]:

time: 270 us -> 268 us (level)
  Pallas kernels: 269 us -> 266 us
where the time goes in v6:
time: 268 us; the launch traced here: 267 us
  Pallas kernels  266 us (99%)
    pallas_call x1, Pallas kernels, device_step(): pl.pallas_call(functools.partial(first_kernel, tp, kvr), out_shape=[full,...  171 us
    pallas_call x1, Pallas kernels, device_step(): pl.pallas_call(functools.partial(second_kernel, tp), out_shape=[V((rows,...  88.5 us
    pallas_call x1, Pallas kernels, device_step(): pl.pallas_call(functools.partial(write_kernel, len(res)), out_shape=[sds(...  6.22 us

profile of v6, /device:TPU:21, one launch (start us, length us, event | category | flops | bytes accessed | tf_op | source)
XLA Modules:
  0.0 267.0 jit_solution(10593948218157539520)
XLA Ops:
  0.6 171.5 %gather_attend_scatter.1 = (bf16[1024,6144]{1,0:T(8,128)(2,1)}, bf16[1024,6144]{1,0:T(8,128)(2,1)}, bf16[8,64,6144]{2,1,0:T(8,128)(2,1)}, bf16[8,64,6144]{2,1,0:...) custom-call(bf16[64,6144]{1,0:T(8,128)(2,1)} %x_hbm.3, ...), custom_call_target="tpu_custom_call" | custom-call | tf_op jit(solution)/shard_map/gather_attend_scatter/pallas_call | solution.py:734
  172.1 88.5 %scatter_grads.1 = (bf16[64,6144]{1,0:T(8,128)(2,1)S(1)}, bf16[64,6144]{1,0:T(8,128)(2,1)S(1)}, f32[1,6144]{1,0:T(1,128)S(1)}, bf16[6144,384]{1,0:T(8,128)(2,1)S...) custom-call(bf16[8,64,6144]{2,1,0:T(8,128)(2,1)} %get-tuple-element.30.dh_own, ...), custom_call_target="tpu_custom_call" | custom-call | tf_op jit(solution)/shard_map/scatter_grads/pallas_call | solution.py:751
  260.6 6.2 %write_results.1 = (bf16[64,6144]{1,0:T(8,128)(2,1)}, bf16[64,6144]{1,0:T(8,128)(2,1)}, f32[1,6144]{1,0:T(1,128)}, bf16[6144,384]{1,0:T(8,128)(2,1)}, f32[6144,1...) custom-call(bf16[64,6144]{1,0:T(8,128)(2,1)S(1)} %get-tuple-element.39.refs_0_, ...), custom_call_target="tpu_custom_call" | custom-call | tf_op jit(solution)/shard_map/write_results/pallas_call | solution.py:764
